TPU v7x, 16 devices: a 4x2x1 block of a 4x4x8 slice. The times are simulated.
16 devices in a mesh: dp: 2 (over y, z), ep: 8 (over x, core).
Axes of the slice: x: 4, y: 2, z: 1, core: 2. Of those that a mesh axis runs over, the one named last changes fastest.
The devices are a block of a 4x4x8 slice.
Arguments:
- x: bfloat16 [48, 64, 2048], P(('dp', 'ep')), parts along dimension 0
- idx: int32 [48, 64, 8], P(('dp', 'ep')), parts along dimension 0
- gates: float32 [48, 64, 8], P(('dp', 'ep')), parts along dimension 0
- g1: float32 [2048], replicated
- wq: bfloat16 [2048, 2048], replicated
- wk: bfloat16 [2048, 2048], replicated
- wv: bfloat16 [2048, 2048], replicated
- wo: bfloat16 [2048, 2048], replicated
- g2: float32 [2048], replicated
- w1: bfloat16 [64, 2048, 1024], P('ep')
- w3: bfloat16 [64, 2048, 1024], P('ep')
- w2: bfloat16 [64, 1024, 2048], P('ep')
Outputs:
- output: bfloat16 [48, 64, 2048], P(('dp', 'ep')), parts along dimension 0
There are 2 independent parts. A program takes and returns all parts, laid end to end along the dimension named above; an argument that names none is the same for every part.
All inputs are finite; a program needn't handle non-finite values.
Results may differ from a plain program's by a relative error of at most 0.0112406.
Values are sent between devices in bfloat16 or wider.
A program may use at most 768 MiB of HBM per device.

v0:
```python
import jax
import jax.numpy as jnp
from jax import lax
from jax.sharding import PartitionSpec as P

EPS = 1e-6
HEAD = 128


def rms(x, g):
    xf = x.astype(jnp.float32)
    return (xf * lax.rsqrt(jnp.mean(xf * xf, axis=-1, keepdims=True) + EPS) * g).astype(jnp.bfloat16)


def attend(q, k, v):
    n = q.shape[0]
    s = jnp.einsum('qhd,khd->hqk', q, k, preferred_element_type=jnp.float32) * q.shape[-1] ** -0.5
    mask = jnp.arange(n)[:, None] >= jnp.arange(n)[None, :]
    s = jnp.where(mask[None], s, -1e30)
    p = jax.nn.softmax(s, axis=-1).astype(jnp.bfloat16)
    return jnp.einsum('hqk,khd->qhd', p, v, preferred_element_type=jnp.float32).astype(jnp.bfloat16)


def slot_pos(flat, n_exp):
    n = flat.shape[0]
    order = jnp.argsort(flat, stable=True)
    se = flat[order]
    counts = jnp.zeros((n_exp,), jnp.int32).at[flat].add(1)
    starts = jnp.cumsum(counts) - counts
    ps = jnp.arange(n, dtype=jnp.int32) - starts[se]
    return jnp.zeros((n,), jnp.int32).at[order].set(ps)


def solution(mesh):
    ep = mesh.shape['ep']
    tok = P(('dp', 'ep'))
    rep = P()
    exs = P('ep')

    def body(x, idx, gates, g1, wq, wk, wv, wo, g2, w1, w3, w2):
        n, s_len, d = x.shape
        t = n * s_len
        top = idx.shape[-1]
        g_loc = w1.shape[0]
        n_exp = g_loc * ep
        avg = top * t // n_exp
        cap = avg + avg // 2
        heads = wq.shape[1] // HEAD
        xf = x.reshape(t, d)
        xn = rms(xf, g1)

        def proj(w):
            return jnp.dot(xn, w, preferred_element_type=jnp.float32).astype(jnp.bfloat16).reshape(n, s_len, heads, HEAD)

        q = proj(wq)
        k = proj(wk)
        v = proj(wv)
        o = lax.map(lambda a: attend(a[0], a[1], a[2]), (q, k, v))
        att = jnp.dot(o.reshape(t, heads * HEAD), wo, preferred_element_type=jnp.float32).astype(jnp.bfloat16)
        h = (xf.astype(jnp.float32) + att.astype(jnp.float32)).astype(jnp.bfloat16)
        z = rms(h, g2)
        flat = idx.reshape(t * top)
        dest = flat * cap + slot_pos(flat, n_exp)
        buf = jnp.zeros((n_exp * cap, d), jnp.bfloat16).at[dest].set(jnp.repeat(z, top, axis=0))
        recv = lax.all_to_all(buf, 'ep', 0, 0, tiled=True)
        r = recv.reshape(ep, g_loc, cap, d).transpose(1, 0, 2, 3).reshape(g_loc, ep * cap, d)
        h1 = jnp.einsum('gnd,gdf->gnf', r, w1, preferred_element_type=jnp.float32)
        h3 = jnp.einsum('gnd,gdf->gnf', r, w3, preferred_element_type=jnp.float32)
        u = (jax.nn.silu(h1) * h3).astype(jnp.bfloat16)
        e_out = jnp.einsum('gnf,gfd->gnd', u, w2, preferred_element_type=jnp.float32).astype(jnp.bfloat16)
        e_out = e_out.reshape(g_loc, ep, cap, d).transpose(1, 0, 2, 3).reshape(ep * g_loc * cap, d)
        back = lax.all_to_all(e_out, 'ep', 0, 0, tiled=True)
        got = back[dest].reshape(t, top, d).astype(jnp.float32)
        moe = jnp.sum(got * gates.reshape(t, top, 1), axis=1)
        y = (h.astype(jnp.float32) + moe).astype(jnp.bfloat16)
        return y.reshape(n, s_len, d)

    return jax.shard_map(body, mesh=mesh, in_specs=(tok, tok, tok, rep, rep, rep, rep, rep, rep, exs, exs, exs), out_specs=tok, check_vma=False)
```

profile of v0, /device:TPU:112, one launch (start us, length us, event | category | flops | bytes accessed | tf_op | source)
XLA Modules:
  0.0 516.6 jit_solution(6590566404462533659)
XLA Ops:
  0.0 0.9 copy.55
  1.0 11.1 %scatter_custom_fusion = s32[64]{0:T(128)S(1)} fusion(s32[1536]{0:T(1024)S(1)} %fusion.37, s32[1536]{0:T(1024)S(1)} %broadcast.231, s32[]{:T(128)} %copy.120), kind=kCustom, calls=%fused_computation.133 | custom fusion | flops 1536 | bytes 260 | tf_op jit(solution)/shard_map/scatter-add | solution.py:28
  15.5 5.0 sort.17
  20.5 8.4 %gather_fusion = s32[1536]{0:T(1024)S(1)} fusion(s32[1536]{0:T(1024)S(1)} %reshape.159, s32[2048]{0:T(1024)S(1)} %pad_clamp_fusion.1), kind=kCustom, calls=%fused_computation | custom fusion | bytes 18432 | tf_op jit(solution)/shard_map/gather | solution.py:27
  28.9 4.5 fusion.36
  33.4 1.1 compare_reduce_fusion.56
  34.5 35.6 %select_subtract_fusion = s32[1536]{0:T(1024)S(1)} fusion(pred[1536]{0:T(1024)(128)(4,1)S(1)} %get-tuple-element.111, pred[1536]{0:T(1024)(128)(4,1)S(1)} %get-tuple-element.110, pred[1536]{0:T(1024)(128)(4,1)S(1)} %get-tuple-element.109, pred[1536]{0:T(1024)(128)(4,1)S(1)} %get-tuple-element.108, pred[1536]{0:T(1024)(128)(4,1)S(1)} %get-tuple-element.107, ...), kind=kLoop, calls=%fused_computation.126 | loop fusion | flops 89088 | bytes 100068 | tf_op jit(solution)/shard_map/sub | solution.py:30
  70.1 6.2 %scatter_custom_fusion.1 = s32[1536]{0:T(1024)S(1)} fusion(s32[1536]{0:T(1024)S(1)} %compare_select_fusion.9, s32[1536]{0:T(1024)S(1)} %select_subtract_fusion, s32[]{:T(128)} %copy.120), kind=kCustom, calls=%fused_computation.129 | custom fusion | bytes 6148 | tf_op jit(solution)/shard_map/scatter | solution.py:31
  76.9 5.4 %fusion.31 = bf16[24,8,16,128]{3,1,2,0:T(8,128)(2,1)S(1)} fusion(bf16[192,2048]{1,0:T(8,128)(2,1)S(1)} %fusion.30, bf16[2048,2048]{1,0:T(8,128)(2,1)} %param.20), kind=kOutput, calls=%fused_computation.52 | convolution fusion | flops 1611005952 | bytes 9961472 | tf_op jit(solution)/shard_map/dot_general | solution.py:53
  82.5 1.9 fusion.32
  84.6 1.1 slice-done.3
  85.7 1.9 fusion.33
  87.7 5.4 %while.10 = (s32[]{:T(128)}, bf16[3,64,16,128]{3,2,1,0:T(8,128)(2,1)}, bf16[3,64,16,128]{3,2,1,0:T(8,128)(2,1)S(1)}, bf16[3,64,16,128]{3,2,1,0:T(8,128)(2,1)S(1)...) while((s32[]{:T(128)}, bf16[3,64,16,128]{3,2,1,0:T(8,128)(2,1)}, bf16[3,64,16,128]{3,2,1,0:T(8,128)(2,1)S(1)}, ...), condition=%wide.region_4.5_spmd, body=%wide.region_1.4_spmd.sunk | while | flops 34149504 | bytes 3949133 | solution.py:58
  88.8 0.9 copy_dynamic-update-slice_fusion.2
  90.5 0.9 copy_dynamic-update-slice_fusion.2
  92.2 0.9 copy_dynamic-update-slice_fusion.2
  93.1 5.7 %multiply_reduce_fusion = (f32[192]{0:T(256)S(1)}, f32[192,2048]{1,0:T(8,128)S(1)}) fusion(bf16[2048,2048]{1,0:T(8,128)(2,1)} %param.21, bf16[24,8,16,128]{3,2,1,0:T(8,128)(2,1)} %bitcast.167, bf16[192,2048]{1,0:T(8,128)(2,1)} %bitcast.160), kind=kOutput, calls=%fused_computation.50 | convolution fusion | flops 1613758208 | bytes 11535104 | tf_op jit(solution)/shard_map/dot_general | solution.py:59
  99.0 14.7 %scatter_custom_fusion.2 = bf16[2304,2048]{1,0:T(8,128)(2,1)} fusion(s32[1536]{0:T(1024)S(1)} %compare_select_fusion.8, bf16[]{:T(256)} %constant.10.clone.1, bf16[192,2048]{1,0:T(8,128)(2,1)S(1)} %multiply_convert_fusion.1), kind=kCustom, calls=%fused_computation.30 | custom fusion | bytes 10223618 | tf_op jit(solution)/shard_map/scatter | solution.py:64
  113.7 112.1 %all_to_all.21 = bf16[8,288,2048]{2,1,0:T(8,128)(2,1)} all-to-all(bf16[8,288,2048]{2,1,0:T(8,128)(2,1)} %bitcast.151), channel_id=1, replica_groups=mesh['dp'=2,'ep'=8] {'ep'}, dimensions={0} | all-to-all | bytes 18874368 | tf_op jit(solution)/shard_map/all_to_all | solution.py:65
  225.8 12.6 %copy.58 = bf16[8,288,2048]{2,0,1:T(8,128)(2,1)} copy(bf16[8,288,2048]{2,1,0:T(8,128)(2,1)} %all_to_all.21) | data formatting | bytes 18874368 | tf_op jit(solution)/shard_map/all_to_all | solution.py:65
  238.4 12.5 %copy.59 = bf16[8,8,36,2048]{3,0,2,1:T(8,128)(2,1)} copy(bf16[8,8,36,2048]{3,1,2,0:T(8,128)(2,1)} %bitcast.152) | data formatting | bytes 18874368 | tf_op jit(solution)/shard_map/transpose | solution.py:66
  250.9 31.0 %fusion.8 = f32[8,288,1024]{2,1,0:T(8,128)} fusion(bf16[8,2048,1024]{2,1,0:T(8,128)(2,1)} %param.24, bf16[8,288,2048]{2,0,1:T(8,128)(2,1)} %bitcast.155), kind=kOutput, calls=%fused_computation.26 | convolution fusion | flops 9663676416 | bytes 52428800 | tf_op jit(solution)/shard_map/gnd,gdf->gnf/dot_general | solution.py:68
  281.9 38.2 %multiply_convert_fusion.clone.6 = bf16[8,288,1024]{2,1,0:T(8,128)(2,1)} fusion(f32[8,288,1024]{2,1,0:T(8,128)} %fusion.8, bf16[8,2048,1024]{2,1,0:T(8,128)(2,1)} %param.23, bf16[8,288,2048]{2,0,1:T(8,128)(2,1)} %bitcast.156), kind=kOutput, calls=%fused_computation.25.clone.clone.clone.clone.clone.1 | convolution fusion | flops 9677832192 | bytes 57147392 | tf_op jit(solution)/shard_map/gnd,gdf->gnf/dot_general | solution.py:67
  320.1 19.5 %fusion.19 = bf16[8,288,2048]{2,1,0:T(8,128)(2,1)} fusion(bf16[8,1024,2048]{2,1,0:T(8,128)(2,1)} %param.25, bf16[8,288,1024]{2,1,0:T(8,128)(2,1)} %multiply_convert_fusion.clone.6), kind=kOutput, calls=%fused_computation.33 | convolution fusion | flops 9668395008 | bytes 47710208 | tf_op jit(solution)/shard_map/gnf,gfd->gnd/dot_general | solution.py:70
  339.6 12.6 %copy.62 = bf16[8,288,2048]{2,0,1:T(8,128)(2,1)} copy(bf16[8,288,2048]{2,1,0:T(8,128)(2,1)} %fusion.19) | data formatting | bytes 18874368 | tf_op jit(solution)/shard_map/convert_element_type | solution.py:70
  352.2 12.5 %copy.63 = bf16[8,8,36,2048]{3,0,2,1:T(8,128)(2,1)} copy(bf16[8,8,36,2048]{3,1,2,0:T(8,128)(2,1)} %bitcast.153) | data formatting | bytes 18874368 | tf_op jit(solution)/shard_map/transpose | solution.py:71
  364.7 12.7 %copy.64 = bf16[8,288,2048]{2,1,0:T(8,128)(2,1)} copy(bf16[8,288,2048]{2,0,1:T(8,128)(2,1)} %bitcast.154) | data formatting | bytes 18874368 | tf_op jit(solution)/shard_map/all_to_all | solution.py:72
  377.4 5.3 %all-to-all-start.1 = ((bf16[8,288,2048]{2,1,0:T(8,128)(2,1)}), bf16[8,288,2048]{2,1,0:T(8,128)(2,1)}, u32[]{:S(2)}, u32[]{:S(2)}) async-start(bf16[8,288,2048]{2,1,0:T(8,128)(2,1)} %copy.64), calls=%async_computation.1 | async-start | bytes 18874368 | tf_op jit(solution)/shard_map/all_to_all | solution.py:72
  382.9 105.5 %all-to-all-done.1 = bf16[8,288,2048]{2,1,0:T(8,128)(2,1)} async-done(((bf16[8,288,2048]{2,1,0:T(8,128)(2,1)}), bf16[8,288,2048]{2,1,0:T(8,128)(2,1)}, u32[]{:S(2)}, u32[]{:S(2)}) %all-to-all-start.1) | async-done | bytes 9437216 | tf_op jit(solution)/shard_map/all_to_all | solution.py:72
  488.4 17.6 %gather_fusion.1 = bf16[1536,2048]{1,0:T(8,128)(2,1)} fusion(bf16[2304,2048]{1,0:T(8,128)(2,1)} %bitcast.79, s32[2048]{0:T(1024)S(1)} %pad_clamp_fusion), kind=kCustom, calls=%fused_computation.1 | custom fusion | bytes 12589056 | tf_op jit(solution)/shard_map/gather | solution.py:73
  506.0 9.2 %fusion.7 = f32[192,2048]{1,0:T(8,128)S(1)} fusion(bf16[1536,2048]{1,0:T(8,128)(2,1)} %gather_fusion.1, f32[192,8]{1,0:T(8,128)S(1)} %bitcast.161), kind=kLoop, calls=%fused_computation.24 | loop fusion | flops 9043968 | bytes 7870464 | tf_op jit(solution)/shard_map/reduce_sum | solution.py:74
  515.3 1.1 add_convert_fusion
  (63 shorter events, 7.3 us)
Async XLA Ops:
  0.0 76.3 %copy-start = (bf16[3,64,2048]{2,1,0:T(8,128)(2,1)S(1)}, bf16[3,64,2048]{2,1,0:T(8,128)(2,1)}, u32[]{:S(2)}) copy-start(bf16[3,64,2048]{2,1,0:T(8,128)(2,1)} %param.14) | copy-start | bytes 2359300
  0.0 76.6 %copy-start.2 = (f32[2048]{0:T(1024)S(1)}, f32[2048]{0:T(1024)}, u32[]{:S(2)}) copy-start(f32[2048]{0:T(1024)} %param.17) | copy-start | bytes 24580
  76.6 5.8 %slice-start = ((s8[8388608]{0:T(1024)(128)(4,1)}), s8[4194304]{0:T(1024)(128)(4,1)S(1)}, s32[]{:S(2)}) async-start(s8[8388608]{0:T(1024)(128)(4,1)} %bitcast.163), calls=%async_computation.2 | async-start | bytes 8388608
  76.9 5.7 %slice-start.1 = ((s8[8388608]{0:T(1024)(128)(4,1)}), s8[4194304]{0:T(1024)(128)(4,1)S(1)}, s32[]{:S(2)}) async-start(s8[8388608]{0:T(1024)(128)(4,1)} %bitcast.163), calls=%async_computation.3 | async-start | bytes 8388608
  82.3 2.3 slice-start.2
  82.5 3.2 slice-start.3
  93.1 5.7 %copy-start.3 = (f32[2048]{0:T(1024)S(1)}, f32[2048]{0:T(1024)}, u32[]{:S(2)}) copy-start(f32[2048]{0:T(1024)} %param.22) | copy-start | bytes 24580
  377.4 5.4 %copy-start.1 = (f32[3,64,8]{1,2,0:T(8,128)S(1)}, f32[3,64,8]{1,2,0:T(8,128)}, u32[]{:S(2)}) copy-start(f32[3,64,8]{1,2,0:T(8,128)} %param.16) | copy-start | bytes 18436
  377.4 111.0 %all-to-all-start.1 = ((bf16[8,288,2048]{2,1,0:T(8,128)(2,1)}), bf16[8,288,2048]{2,1,0:T(8,128)(2,1)}, u32[]{:S(2)}, u32[]{:S(2)}) async-start(bf16[8,288,2048]{2,1,0:T(8,128)(2,1)} %copy.64), calls=%async_computation.1 | async-start | bytes 18874368 | tf_op jit(solution)/shard_map/all_to_all | solution.py:72
where the time goes:
time: 526 us; the launch traced here: 517 us
  local copies, waits for them, and re-layouts  119 us (23%)
  blocking collectives  112 us (21%)
  matrix products  105 us (20%)
  waiting for transfers between devices  105 us (20%)
  other arithmetic  69.1 us (13%)
  starting transfers between devices  5.35 us (1%)
    all_to_all x1, blocking collectives, body(): recv = lax.all_to_all(buf, 'ep', 0, 0, tiled=True)  112 us
    all_to_all x1, waiting for transfers between devices, body(): back = lax.all_to_all(e_out, 'ep', 0, 0, tiled=True)  105 us
    dot_general x1, matrix products, body(): h1 = jnp.einsum('gnd,gdf->gnf', r, w1, preferred_element_type=jnp.float32)  38.2 us
    sub x1, other arithmetic, slot_pos(): ps = jnp.arange(n, dtype=jnp.int32) - starts[se]  35.6 us
    dot_general x1, matrix products, body(): h3 = jnp.einsum('gnd,gdf->gnf', r, w3, preferred_element_type=jnp.float32)  31 us
    dot_general x1, matrix products, body(): jnp.einsum('gnf,gfd->gnd', u, w2, preferred_element_type=jnp.float32)  19.5 us
    gather x1, local copies, waits for them, and re-layouts, body(): got = back[dest].reshape(t, top, d).astype(jnp.float32)  17.6 us
    scatter x1, local copies, waits for them, and re-layouts, body(): jnp.zeros((n_exp * cap, d), jnp.bfloat16).at[dest]  14.7 us
  transfers between devices with their start and end apart: 1, of which 1 were waited for; matrix products, arithmetic and copies ran while one was open for 0% of the time, Pallas kernels for 0%

commit v1 on v0

v1 whole, which is shorter than its diff:
```python
import functools

import jax
import jax.numpy as jnp
from jax import lax
from jax.experimental import pallas as pl
from jax.experimental.pallas import tpu as pltpu
from jax.sharding import PartitionSpec as P

EPS = 1e-6
HEAD = 128
F32, BF16 = jnp.float32, jnp.bfloat16


def rms(xf, g):
    return (xf * lax.rsqrt(jnp.mean(xf * xf, axis=-1, keepdims=True) + EPS) * g).astype(BF16)


def attn_kernel(hb, seq, x_ref, g1_ref, g2_ref, wq_ref, wk_ref, wv_ref, wo_ref, h_ref, z_ref, xn_ref, acc_ref):
    i = pl.program_id(0)
    t = x_ref.shape[0]

    @pl.when(i == 0)
    def _():
        xn_ref[...] = rms(x_ref[...].astype(F32), g1_ref[...])
        acc_ref[...] = jnp.zeros_like(acc_ref)

    xn = xn_ref[...]
    q = jnp.dot(xn, wq_ref[...], preferred_element_type=F32).astype(BF16)
    k = jnp.dot(xn, wk_ref[...], preferred_element_type=F32).astype(BF16)
    v = jnp.dot(xn, wv_ref[...], preferred_element_type=F32).astype(BF16)
    row = lax.broadcasted_iota(jnp.int32, (t, t), 0)
    col = lax.broadcasted_iota(jnp.int32, (t, t), 1)
    mask = (row >= col) & (row // seq == col // seq)
    outs = []
    for j in range(hb):
        sl = slice(j * HEAD, (j + 1) * HEAD)
        s = lax.dot_general(q[:, sl], k[:, sl], (((1,), (1,)), ((), ())), preferred_element_type=F32) * HEAD ** -0.5
        s = jnp.where(mask, s, -1e30)
        e = jnp.exp(s - jnp.max(s, axis=-1, keepdims=True))
        p = (e / jnp.sum(e, axis=-1, keepdims=True)).astype(BF16)
        outs.append(jnp.dot(p, v[:, sl], preferred_element_type=F32).astype(BF16))
    o = jnp.concatenate(outs, axis=1)
    acc_ref[...] += jnp.dot(o, wo_ref[...], preferred_element_type=F32)

    @pl.when(i == pl.num_programs(0) - 1)
    def _():
        att = acc_ref[...].astype(BF16)
        h = (x_ref[...].astype(F32) + att.astype(F32)).astype(BF16)
        h_ref[...] = h
        z_ref[...] = rms(h.astype(F32), g2_ref[...])


def attention(xf, g1, g2, wq, wk, wv, wo, seq, hb=2):
    t, d = xf.shape
    wid = wq.shape[1]
    c = hb * HEAD
    return pl.pallas_call(
        functools.partial(attn_kernel, hb, seq),
        grid=(wid // c,),
        in_specs=[
            pl.BlockSpec((t, d), lambda i: (0, 0)),
            pl.BlockSpec((1, d), lambda i: (0, 0)),
            pl.BlockSpec((1, d), lambda i: (0, 0)),
            pl.BlockSpec((d, c), lambda i: (0, i)),
            pl.BlockSpec((d, c), lambda i: (0, i)),
            pl.BlockSpec((d, c), lambda i: (0, i)),
            pl.BlockSpec((c, d), lambda i: (i, 0)),
        ],
        out_specs=[pl.BlockSpec((t, d), lambda i: (0, 0))] * 2,
        out_shape=[jax.ShapeDtypeStruct((t, d), BF16)] * 2,
        scratch_shapes=[pltpu.VMEM((t, d), BF16), pltpu.VMEM((t, d), F32)],
        compiler_params=pltpu.CompilerParams(dimension_semantics=("arbitrary",), vmem_limit_bytes=48 * 2**20),
        cost_estimate=pl.CostEstimate(flops=8 * t * d * wid, bytes_accessed=8 * d * wid, transcendentals=0),
        name="attention",
    )(xf, g1.reshape(1, d), g2.reshape(1, d), wq, wk, wv, wo)


def split3(g):
    hi = lax.reduce_precision(g, 8, 7)
    mid = lax.reduce_precision(g - hi, 8, 7)
    return hi, mid, g - hi - mid


def solution(mesh):
    ep = mesh.shape['ep']
    tok = P(('dp', 'ep'))
    rep = P()
    exs = P('ep')

    def body(x, idx, gates, g1, wq, wk, wv, wo, g2, w1, w3, w2):
        n, s_len, d = x.shape
        t = n * s_len
        top = idx.shape[-1]
        g_loc = w1.shape[0]
        avg = top * t // (g_loc * ep)
        cap = avg + avg // 2
        h, z = attention(x.reshape(t, d), g1, g2, wq, wk, wv, wo, s_len)

        meta = jnp.concatenate([idx.reshape(t, top).astype(F32), gates.reshape(t, top)], axis=1)
        meta = lax.all_gather(meta, 'ep')
        ids, gt = meta[..., :top], meta[..., top:]
        mine = (lax.axis_index('ep') * g_loc + jnp.arange(g_loc)).astype(F32)
        hit = ids[:, :, :, None] == mine
        mask = jnp.any(hit, axis=2)
        gate = jnp.sum(jnp.where(hit, gt[:, :, :, None], 0.0), axis=2)
        tri = (jnp.arange(t)[:, None] > jnp.arange(t)[None, :]).astype(BF16)
        rank = jnp.einsum('ut,ste->sue', tri, mask.astype(BF16), preferred_element_type=F32)
        place = jnp.where(mask, rank, -1.0)
        sel = place[..., None] == jnp.arange(cap, dtype=F32)
        sel = sel.reshape(ep, t, g_loc * cap)
        gate = jnp.broadcast_to(gate[..., None], gate.shape + (cap,)).reshape(sel.shape)
        zs = lax.all_gather(z, 'ep')
        r = jnp.einsum('str,std->srd', sel.astype(BF16), zs, preferred_element_type=F32).astype(BF16)
        r = r.reshape(ep, g_loc, cap, d).transpose(1, 0, 2, 3).reshape(g_loc, ep * cap, d)
        h1 = jnp.einsum('gnd,gdf->gnf', r, w1, preferred_element_type=F32)
        h3 = jnp.einsum('gnd,gdf->gnf', r, w3, preferred_element_type=F32)
        u = (jax.nn.silu(h1) * h3).astype(BF16)
        e_out = jnp.einsum('gnf,gfd->gnd', u, w2, preferred_element_type=F32).astype(BF16)
        e_out = e_out.reshape(g_loc, ep, cap, d).transpose(1, 0, 2, 3).reshape(ep, g_loc * cap, d)
        comb = jnp.concatenate([jnp.where(sel, p, 0.0).astype(BF16) for p in split3(gate)], axis=1)
        part = jnp.einsum('sqr,srd->sqd', comb, e_out, preferred_element_type=F32)
        part = part.reshape(ep, 3, t, d).sum(axis=1)
        moe = lax.psum_scatter(part, 'ep', scatter_dimension=0)
        y = (h.astype(F32) + moe).astype(BF16)
        return y.reshape(n, s_len, d)

    return jax.shard_map(body, mesh=mesh, in_specs=(tok, tok, tok, rep, rep, rep, rep, rep, rep, exs, exs, exs), out_specs=tok, check_vma=False)
```

time: 526 us -> 343 us (0.65); the launches traced: 517 us -> 339 us
  blocking collectives: 112 us -> 24.9 us
  local copies, waits for them, and re-layouts: 119 us -> 53.5 us
  other arithmetic: 69.1 us -> 26.6 us
  waiting for transfers between devices: 105 us -> 78 us
  Pallas kernels: 0 us -> 20.4 us
  matrix products: 105 us -> 122 us
  between operations: 0.46 us -> 13.8 us
  starting transfers between devices: 5.35 us -> 0.07 us
    all_to_all x1 -> x0, blocking collectives: 112 us -> none  [body(): recv = lax.all_to_all(buf, 'ep', 0, 0, tiled=True)]
    all_to_all x1 -> x0, waiting for transfers between devices: 105 us -> none  [body(): back = lax.all_to_all(e_out, 'ep', 0, 0, tiled=True)]
    reduce_scatter x0 -> x1, waiting for transfers between devices: none -> 68.7 us  [body(): moe = lax.psum_scatter(part, 'ep', scatter_dimension=0)]
    sub x5 -> x0, other arithmetic: 36 us -> none  [the longest x1 35.6 us: slot_pos(): ps = jnp.arange(n, dtype=jnp.int32) - starts[se]]
    gather x6 -> x0, local copies, waits for them, and re-layouts: 28.8 us -> none  [the longest x1 17.6 us: body(): got = back[dest].reshape(t, top, d).astype(jnp.float32)]
    all_to_all x2 -> x0, local copies, waits for them, and re-layouts: 25.3 us -> none  [the longest x1 12.7 us: body(): back = lax.all_to_all(e_out, 'ep', 0, 0, tiled=True)]
    all_gather x0 -> x1, blocking collectives: none -> 24.9 us  [body(): meta = lax.all_gather(meta, 'ep')]
    scatter x2 -> x0, local copies, waits for them, and re-layouts: 20.9 us -> none  [the longest x1 14.7 us: body(): jnp.zeros((n_exp * cap, d), jnp.bfloat16).at[dest]]
  transfers between devices with their start and end apart: 1 -> 2, of which waited for: 1 -> 2; matrix products, arithmetic and copies ran while one was open for 0% -> 2% of each run, Pallas kernels for 0% -> 0%
where the time goes in v1:
time: 343 us; the launch traced here: 339 us
  matrix products  122 us (36%)
  waiting for transfers between devices  78 us (23%)
  local copies, waits for them, and re-layouts  53.5 us (16%)
  other arithmetic  26.6 us (8%)
  blocking collectives  24.9 us (7%)
  Pallas kernels  20.4 us (6%)
  between operations  13.8 us (4%)
    reduce_scatter x1, waiting for transfers between devices, body(): moe = lax.psum_scatter(part, 'ep', scatter_dimension=0)  68.7 us
    dot_general x1, matrix products, body(): h1 = jnp.einsum('gnd,gdf->gnf', r, w1, preferred_element_type=F32)  38.2 us
    dot_general x1, matrix products, body(): h3 = jnp.einsum('gnd,gdf->gnf', r, w3, preferred_element_type=F32)  31 us
    all_gather x1, blocking collectives, body(): meta = lax.all_gather(meta, 'ep')  24.9 us
    dot_general x1, matrix products, body(): part = jnp.einsum('sqr,srd->sqd', comb, e_out, preferred_element_type=F32)  24.4 us
    pallas_call x1, Pallas kernels, attention(): pl.pallas_call(functools.partial(attn_kernel, hb, seq), grid=(wid // c,),...  20.4 us
    dot_general x1, matrix products, body(): jnp.einsum('gnf,gfd->gnd', u, w2, preferred_element_type=F32).astype(BF16)  19.3 us
    reduce_sum x1, other arithmetic, body(): part = part.reshape(ep, 3, t, d).sum(axis=1)  19.2 us
  transfers between devices with their start and end apart: 2, of which 2 were waited for; matrix products, arithmetic and copies ran while one was open for 2% of the time, Pallas kernels for 0%

profile of v1, /device:TPU:112, one launch (start us, length us, event | category | flops | bytes accessed | tf_op | source)
XLA Modules:
  0.0 339.5 jit_solution(15524219747769435690)
XLA Ops:
  6.5 0.0 all-gather.5.cloned.1.call-start
  6.6 1.1 copy-done
  7.7 0.7 copy-done.1
  8.4 0.7 copy-done.2
  9.1 20.4 %attention.1 = (bf16[192,2048]{1,0:T(8,128)(2,1)S(1)}, bf16[192,2048]{1,0:T(8,128)(2,1)}) custom-call(bf16[192,2048]{1,0:T(8,128)(2,1)S(1)} %bitcast.44, f32[1,2048]{1,0:T(1,128)S(1)} %bitcast.45, f32[1,2048]{1,0:T(1,128)S(1)} %bitcast.46, bf16[2048,2048]{1,0:T(8,128)(2,1)} %wq_ref.1, bf16[2048,2048]{1,0:T(8,128)(2,1)} %wk_ref.1, bf16[2048,2048]{1,0:T(8,128)(2,1)} %wv_ref.1, ...), custom_call_target="tpu_custom_call" | custom-call | flops 6442450944 | bytes 33554432 | tf_op jit(solution)/shard_map/attention/pallas_call | solution.py:58
  29.5 0.1 all-gather.5.cloned.1.call-update
  29.6 0.1 reduce-scatter.2.cloned.1.call-start
  29.7 0.1 eq.39
  29.8 0.1 convert_element_type.42
  29.9 0.1 reshape.50
  30.0 24.9 %all-gather.2 = f32[8,192,16]{1,2,0:T(8,128)S(1)} all-gather(f32[1,192,16]{1,2,0:T(8,128)S(1)} %maximum_bitcast_fusion), channel_id=2, replica_groups=mesh['dp'=2,'ep'=8] {'ep'}, dimensions={0}, use_global_device_ids=true | all-gather | bytes 110592 | tf_op jit(solution)/shard_map/all_gather | solution.py:101
  54.9 0.1 fusion.26
  55.1 0.1 compare_reduce_fusion
  55.2 0.2 fusion.25
  55.4 0.2 eq.36
  55.6 0.2 broadcast_in_dim.38
  55.8 2.0 fusion.20
  57.8 2.6 fusion.21
  60.4 9.3 %all-gather.5.cloned.1.call-done = bf16[1536,2048]{1,0:T(8,128)(2,1)} async-done(((bf16[192,2048]{1,0:T(8,128)(2,1)}), bf16[1536,2048]{1,0:T(8,128)(2,1)}) %all-gather.5.cloned.1.call-update) | async-done | bytes 6291472 | tf_op jit(solution)/shard_map/all_gather | solution.py:113
  69.7 9.0 %convolution_convert_fusion = bf16[8,288,2048]{2,1,0:T(8,128)(2,1)} fusion(pred[8,192,288]{1,2,0:T(32,128)(4,1)S(1)} %get-tuple-element.10, bf16[8,192,2048]{2,1,0:T(8,128)(2,1)} %bitcast.53), kind=kOutput, calls=%fused_computation.9 | convolution fusion | flops 1816657920 | bytes 16171008 | tf_op jit(solution)/shard_map/str,std->srd/dot_general | solution.py:114
  78.7 12.7 %copy.51 = bf16[8,288,2048]{2,0,1:T(8,128)(2,1)} copy(bf16[8,288,2048]{2,1,0:T(8,128)(2,1)} %convolution_convert_fusion) | data formatting | bytes 18874368 | tf_op jit(solution)/shard_map/convert_element_type | solution.py:114
  91.5 12.5 %copy.52 = bf16[8,8,36,2048]{3,0,2,1:T(8,128)(2,1)} copy(bf16[8,8,36,2048]{3,1,2,0:T(8,128)(2,1)} %bitcast.48) | data formatting | bytes 18874368 | tf_op jit(solution)/shard_map/transpose | solution.py:115
  104.0 31.0 %fusion.2 = f32[8,288,1024]{2,1,0:T(8,128)} fusion(bf16[8,2048,1024]{2,1,0:T(8,128)(2,1)} %param.22, bf16[8,288,2048]{2,0,1:T(8,128)(2,1)} %bitcast.54), kind=kOutput, calls=%fused_computation.3 | convolution fusion | flops 9663676416 | bytes 52428800 | tf_op jit(solution)/shard_map/gnd,gdf->gnf/dot_general | solution.py:117
  135.0 38.2 %multiply_convert_fusion.clone.6 = bf16[8,288,1024]{2,1,0:T(8,128)(2,1)} fusion(f32[8,288,1024]{2,1,0:T(8,128)} %fusion.2, bf16[8,2048,1024]{2,1,0:T(8,128)(2,1)} %param.21, bf16[8,288,2048]{2,0,1:T(8,128)(2,1)} %bitcast.55), kind=kOutput, calls=%fused_computation.2.clone.clone.clone.clone.clone.1 | convolution fusion | flops 9677832192 | bytes 57147392 | tf_op jit(solution)/shard_map/gnd,gdf->gnf/dot_general | solution.py:116
  173.2 19.3 %fusion.11 = bf16[8,288,2048]{2,1,0:T(8,128)(2,1)} fusion(bf16[8,1024,2048]{2,1,0:T(8,128)(2,1)} %param.23, bf16[8,288,1024]{2,1,0:T(8,128)(2,1)} %multiply_convert_fusion.clone.6), kind=kOutput, calls=%fused_computation.8 | convolution fusion | flops 9668395008 | bytes 47710208 | tf_op jit(solution)/shard_map/gnf,gfd->gnd/dot_general | solution.py:119
  192.5 12.5 %copy.55 = bf16[8,288,2048]{2,0,1:T(8,128)(2,1)} copy(bf16[8,288,2048]{2,1,0:T(8,128)(2,1)} %fusion.11) | data formatting | bytes 18874368 | tf_op jit(solution)/shard_map/convert_element_type | solution.py:119
  205.1 12.5 %copy.56 = bf16[8,8,36,2048]{3,0,2,1:T(8,128)(2,1)} copy(bf16[8,8,36,2048]{3,1,2,0:T(8,128)(2,1)} %bitcast.49) | data formatting | bytes 18874368 | tf_op jit(solution)/shard_map/transpose | solution.py:120
  217.6 24.4 %fusion = f32[8,576,2048]{2,1,0:T(8,128)} fusion(bf16[8,288,2048]{2,0,1:T(8,128)(2,1)} %bitcast.50, bf16[8,192,288]{1,2,0:T(8,128)(2,1)} %get-tuple-element.12, bf16[8,192,288]{1,2,0:T(8,128)(2,1)} %get-tuple-element.11, bf16[8,192,288]{1,2,0:T(8,128)(2,1)S(1)} %get-tuple-element.9), kind=kOutput, calls=%fused_computation | convolution fusion | flops 5443780608 | bytes 49840128 | tf_op jit(solution)/shard_map/sqr,srd->sqd/dot_general | solution.py:122
  242.0 19.2 %reduce_sum.19 = f32[8,192,2048]{2,1,0:T(8,128)} reduce(f32[8,3,192,2048]{3,2,1,0:T(8,128)} %bitcast.47, f32[]{:T(128)} %constant.5.clone.1), dimensions={1}, to_apply=%region_2.3 | reduce | flops 6291456 | bytes 50331652 | tf_op jit(solution)/shard_map/reduce_sum | solution.py:123
  261.2 0.1 reduce-scatter.2.cloned.1.call-update
  261.2 68.7 %reduce-scatter.2.cloned.1.call-done = f32[1,192,2048]{2,1,0:T(8,128)} async-done(((f32[8,192,2048]{2,1,0:T(8,128)}), f32[1,192,2048]{2,1,0:T(8,128)}) %reduce-scatter.2.cloned.1.call-update) | async-done | bytes 1572880 | tf_op jit(solution)/shard_map/reduce_scatter | solution.py:124
  329.9 2.5 fusion.24
  (16 shorter events, 0.1 us)
Async XLA Ops:
  6.5 63.2 %all-gather.5.cloned.1.call-start = ((), (), s32[]{:S(2)}) async-start(), calls=%async_computation.2 | async-start | bytes 7077888 | tf_op jit(solution)/shard_map/all_gather | solution.py:113
  6.6 1.1 copy-start
  7.7 0.7 copy-start.1
  8.4 0.7 copy-start.2
  9.1 20.7 %copy-start.4 = (s32[3,64,8]{1,2,0:T(8,128)S(1)}, s32[3,64,8]{1,2,0:T(8,128)}, u32[]{:S(2)}) copy-start(s32[3,64,8]{1,2,0:T(8,128)} %param.13) | copy-start | bytes 18436
  9.1 20.8 %copy-start.3 = (f32[3,64,8]{1,2,0:T(8,128)S(1)}, f32[3,64,8]{1,2,0:T(8,128)}, u32[]{:S(2)}) copy-start(f32[3,64,8]{1,2,0:T(8,128)} %param.14) | copy-start | bytes 18436
  29.6 300.3 %reduce-scatter.2.cloned.1.call-start = ((), (), s32[]{:S(2)}) async-start(), calls=%async_computation.1 | async-start | bytes 14155776 | tf_op jit(solution)/shard_map/reduce_scatter | solution.py:124
Sparse Core Ops, SparseCore 0:
  29.7 39.9 all-gather.4
  261.4 68.4 reduce-scatter.1

commit v2 on v1

v2 whole, which is shorter than its diff:
```python
import functools

import jax
import jax.numpy as jnp
from jax import lax
from jax.experimental import pallas as pl
from jax.experimental.pallas import tpu as pltpu
from jax.sharding import PartitionSpec as P

EPS = 1e-6
HEAD = 128
F32, BF16 = jnp.float32, jnp.bfloat16


def rms(xf, g):
    return (xf * lax.rsqrt(jnp.mean(xf * xf, axis=-1, keepdims=True) + EPS) * g).astype(BF16)


def attn_kernel(hb, seq, x_ref, g1_ref, g2_ref, wq_ref, wk_ref, wv_ref, wo_ref, h_ref, z_ref, xn_ref, acc_ref):
    i = pl.program_id(0)
    t = x_ref.shape[0]

    @pl.when(i == 0)
    def _():
        xn_ref[...] = rms(x_ref[...].astype(F32), g1_ref[...])
        acc_ref[...] = jnp.zeros_like(acc_ref)

    xn = xn_ref[...]
    q = jnp.dot(xn, wq_ref[...], preferred_element_type=F32).astype(BF16)
    k = jnp.dot(xn, wk_ref[...], preferred_element_type=F32).astype(BF16)
    v = jnp.dot(xn, wv_ref[...], preferred_element_type=F32).astype(BF16)
    row = lax.broadcasted_iota(jnp.int32, (t, t), 0)
    col = lax.broadcasted_iota(jnp.int32, (t, t), 1)
    mask = (row >= col) & (row // seq == col // seq)
    outs = []
    for j in range(hb):
        sl = slice(j * HEAD, (j + 1) * HEAD)
        s = lax.dot_general(q[:, sl], k[:, sl], (((1,), (1,)), ((), ())), preferred_element_type=F32) * HEAD ** -0.5
        s = jnp.where(mask, s, -1e30)
        e = jnp.exp(s - jnp.max(s, axis=-1, keepdims=True))
        p = (e / jnp.sum(e, axis=-1, keepdims=True)).astype(BF16)
        outs.append(jnp.dot(p, v[:, sl], preferred_element_type=F32).astype(BF16))
    o = jnp.concatenate(outs, axis=1)
    acc_ref[...] += jnp.dot(o, wo_ref[...], preferred_element_type=F32)

    @pl.when(i == pl.num_programs(0) - 1)
    def _():
        att = acc_ref[...].astype(BF16)
        h = (x_ref[...].astype(F32) + att.astype(F32)).astype(BF16)
        h_ref[...] = h
        z = rms(h.astype(F32), g2_ref[...])
        kc = z_ref.shape[2]
        for c in range(z_ref.shape[0]):
            z_ref[c] = z[:, c * kc:(c + 1) * kc]


def attention(xf, g1, g2, wq, wk, wv, wo, seq, nz, hb=2):
    t, d = xf.shape
    wid = wq.shape[1]
    c = hb * HEAD
    return pl.pallas_call(
        functools.partial(attn_kernel, hb, seq),
        grid=(wid // c,),
        in_specs=[
            pl.BlockSpec((t, d), lambda i: (0, 0)),
            pl.BlockSpec((1, d), lambda i: (0, 0)),
            pl.BlockSpec((1, d), lambda i: (0, 0)),
            pl.BlockSpec((d, c), lambda i: (0, i)),
            pl.BlockSpec((d, c), lambda i: (0, i)),
            pl.BlockSpec((d, c), lambda i: (0, i)),
            pl.BlockSpec((c, d), lambda i: (i, 0)),
        ],
        out_specs=[pl.BlockSpec((t, d), lambda i: (0, 0)), pl.BlockSpec((nz, t, d // nz), lambda i: (0, 0, 0))],
        out_shape=[jax.ShapeDtypeStruct((t, d), BF16), jax.ShapeDtypeStruct((nz, t, d // nz), BF16)],
        scratch_shapes=[pltpu.VMEM((t, d), BF16), pltpu.VMEM((t, d), F32)],
        compiler_params=pltpu.CompilerParams(dimension_semantics=("arbitrary",), vmem_limit_bytes=48 * 2**20),
        cost_estimate=pl.CostEstimate(flops=8 * t * d * wid, bytes_accessed=8 * d * wid, transcendentals=0),
        name="attention",
    )(xf, g1.reshape(1, d), g2.reshape(1, d), wq, wk, wv, wo)


MESH = pl.DeviceIdType.MESH
NZ, NW, NW2, NCOL = 4, 4, 8, 256


def moe_kernel(ep, cfg, meta_ref, z_ref, h_ref, w1_ref, w3_ref, w2_ref, y_ref,
               mbuf, zbuf, dbuf, gbuf, wbuf, acc1, acc3, rbuf, ubuf, w2buf, ebuf, h1buf, h2buf,
               load_sem, m_send, m_recv, z_send, z_recv, w_sem, w2_sem, r_send, r_recv, ready):
    g_loc, cp, ncol = cfg
    nz, _, t, kc = zbuf.shape
    tp = mbuf.shape[2]
    ff = acc1.shape[2]
    d = nz * kc
    rows = ep * cp
    chips = ep // 2
    half = t // 2
    n2 = d // ncol
    nq = ff // ncol
    nw, nw2 = wbuf.shape[0], w2buf.shape[0]

    me = lax.axis_index('ep')
    chip, core = me // 2, lax.rem(me, 2)
    rchip, lchip, ochip = lax.rem(chip + 1, chips), lax.rem(chip + chips - 1, chips), lax.rem(chip + 2, chips)
    right, left, opp, sib = rchip * 2 + core, lchip * 2 + core, ochip * 2 + core, chip * 2 + 1 - core

    def send(src, dst, ssem, rsem, dev):
        return pltpu.make_async_remote_copy(src_ref=src, dst_ref=dst, send_sem=ssem, recv_sem=rsem,
                                            device_id={'ep': dev}, device_id_type=MESH)

    def wcopy(n, which):
        e, c = lax.rem(n, g_loc), n // g_loc
        ref = w3_ref if which else w1_ref
        slot = lax.rem(n, nw)
        return pltpu.make_async_copy(ref.at[e, pl.ds(c * kc, kc)], wbuf.at[slot, which], w_sem.at[slot, which])

    def w2copy(n):
        e, c = lax.rem(n, g_loc), n // g_loc
        slot = lax.rem(n, nw2)
        return pltpu.make_async_copy(w2_ref.at[e, :, pl.ds(pl.multiple_of(c * ncol, ncol), ncol)], w2buf.at[slot], w2_sem.at[slot])

    zload = pltpu.make_async_copy(z_ref, zbuf.at[:, me], load_sem.at[0])
    mload = pltpu.make_async_copy(meta_ref, mbuf.at[me], load_sem.at[1])
    zload.start()
    mload.start()
    for n in range(nw):
        wcopy(n, 0).start()
        wcopy(n, 1).start()
    for n in range(nw2):
        w2copy(n).start()

    barrier = pltpu.get_barrier_semaphore()
    for dev in (right, left, sib):
        pl.semaphore_signal(barrier, inc=1, device_id={'ep': dev}, device_id_type=MESH)
    pl.semaphore_wait(barrier, 3)

    def mcopy(k):
        who, dev = ((me, right), (me, left), (me, sib), (left, right), (left, sib), (right, sib), (opp, sib))[k]
        return send(mbuf.at[who], mbuf.at[who], m_send.at[k], m_recv.at[k], dev)

    def zcopy(c, k):
        if k == 3:
            ref, dev = zbuf.at[c, left, pl.ds(0, half)], right
        elif k == 4:
            ref, dev = zbuf.at[c, right, pl.ds(half, half)], left
        else:
            who, dev = {0: (me, right), 1: (me, left), 2: (me, sib), 5: (left, sib), 6: (right, sib), 7: (opp, sib)}[k]
            ref = zbuf.at[c, who]
        return send(ref, ref, z_send.at[c, k], z_recv.at[c, k], dev)

    def own(c):
        for k in (0, 1, 2):
            zcopy(c, k).start()

    def stage1(c):
        zcopy(c, 0).wait_recv()
        zcopy(c, 3).start()
        zcopy(c, 5).start()
        zcopy(c, 1).wait_recv()
        zcopy(c, 4).start()
        zcopy(c, 6).start()

    def stage2(c):
        zcopy(c, 3).wait_recv()
        zcopy(c, 4).wait_recv()
        zcopy(c, 7).start()

    def stage3(c):
        for k in (2, 5, 6, 7):
            zcopy(c, k).wait_recv()

    mload.wait()
    for k in (0, 1, 2):
        mcopy(k).start()
    zload.wait()
    own(0)

    def zero(e, _):
        acc1[e] = jnp.zeros_like(acc1[e])
        acc3[e] = jnp.zeros_like(acc3[e])
        return 0

    lax.fori_loop(0, g_loc, zero, 0)
    mcopy(0).wait_recv()
    mcopy(3).start()
    mcopy(4).start()
    mcopy(1).wait_recv()
    mcopy(5).start()
    own(1)
    mcopy(3).wait_recv()
    mcopy(6).start()
    for k in (2, 4, 5, 6):
        mcopy(k).wait_recv()

    base = (me * g_loc).astype(F32)

    def build(s, _):
        m = mbuf[s]
        top = m.shape[0] // 2
        ids, gt = m[:top], m[top:]
        masks, gates = [], []
        for e in range(g_loc):
            hit = ids == base + float(e)
            masks.append(jnp.max(jnp.where(hit, 1.0, 0.0), axis=0, keepdims=True))
            gates.append(jnp.sum(jnp.where(hit, gt, 0.0), axis=0, keepdims=True))
        mask, gate = jnp.concatenate(masks, axis=0), jnp.concatenate(gates, axis=0)
        before = lax.broadcasted_iota(jnp.int32, (tp, tp), 0) < lax.broadcasted_iota(jnp.int32, (tp, tp), 1)
        rank = jnp.dot(mask.astype(BF16), jnp.where(before, 1.0, 0.0).astype(BF16), preferred_element_type=F32)
        place = jnp.where(mask > 0.5, rank, -1.0)
        slot = lax.broadcasted_iota(jnp.int32, (cp, t), 0).astype(F32)
        dbuf[s] = jnp.concatenate([jnp.where(slot == place[e:e + 1, :t], 1.0, 0.0) for e in range(g_loc)], axis=0).astype(BF16)
        re = lax.broadcasted_iota(jnp.int32, (g_loc, g_loc * cp), 0)
        rr = lax.broadcasted_iota(jnp.int32, (g_loc, g_loc * cp), 1)
        spread = jnp.where((rr >= re * cp) & (rr < re * cp + cp), 1.0, 0.0).astype(BF16)

        def widen(a):
            return lax.dot_general(a, spread, (((0,), (0,)), ((), ())), preferred_element_type=F32)[:t]

        slots = lax.rem(lax.broadcasted_iota(jnp.int32, (t, g_loc * cp), 1), cp).astype(F32)
        sel = widen(place.astype(BF16)) == slots
        hi = gate.astype(BF16)
        r1 = gate - hi.astype(F32)
        mid = r1.astype(BF16)
        lo = (r1 - mid.astype(F32)).astype(BF16)
        for i, part in enumerate((hi, mid, lo)):
            gbuf[s, i * t:(i + 1) * t] = jnp.where(sel, widen(part), 0.0).astype(BF16)
        return 0

    stage1(0)
    lax.fori_loop(0, ep // 2, build, 0)
    stage2(0)
    lax.fori_loop(ep // 2, ep, build, 0)

    def dispatch(c):
        def pair(p, _):
            a = jnp.dot(dbuf[2 * p], zbuf[c, 2 * p], preferred_element_type=F32)
            b = jnp.dot(dbuf[2 * p + 1], zbuf[c, 2 * p + 1], preferred_element_type=F32)
            for e in range(g_loc):
                sl = slice(e * cp, (e + 1) * cp)
                rbuf[e, pl.ds(pl.multiple_of(p * 2 * cp, 2 * cp), 2 * cp)] = jnp.concatenate([a[sl], b[sl]], axis=0).astype(BF16)
            return 0

        lax.fori_loop(0, ep // 2, pair, 0)

    def expert_in(c, last):
        def step(e, _):
            n = c * g_loc + e
            slot = lax.rem(n, nw)
            wcopy(n, 0).wait()
            wcopy(n, 1).wait()
            r = rbuf[e]
            a = acc1[e] + jnp.dot(r, wbuf[slot, 0], preferred_element_type=F32)
            b = acc3[e] + jnp.dot(r, wbuf[slot, 1], preferred_element_type=F32)
            if last:
                ubuf[e] = (a / (1.0 + jnp.exp(-a)) * b).astype(BF16)
            else:
                acc1[e] = a
                acc3[e] = b

            @pl.when(n + nw < nz * g_loc)
            def _():
                wcopy(n + nw, 0).start()
                wcopy(n + nw, 1).start()

            return 0

        return step

    def chunk(c, _):
        stage3(c)
        dispatch(c)

        @pl.when(c + 2 < nz)
        def _():
            own(c + 2)

        stage1(c + 1)
        step = expert_in(c, False)
        lax.fori_loop(0, g_loc // 2, step, 0)
        stage2(c + 1)
        lax.fori_loop(g_loc // 2, g_loc, step, 0)
        return 0

    lax.fori_loop(0, nz - 1, chunk, 0)
    stage3(nz - 1)
    dispatch(nz - 1)
    lax.fori_loop(0, g_loc, expert_in(nz - 1, True), 0)
    pl.semaphore_signal(ready, inc=1, device_id={'ep': sib}, device_id_type=MESH)

    def cols(c):
        return pl.ds(pl.multiple_of(lax.rem(c, nq) * ncol, ncol), ncol)

    def rcopy(c, k):
        if k == 0:
            src = acc1.at[pl.ds(chips, chips), pl.ds(0, t), cols(c)]
            dst, dev = acc3.at[pl.ds(c // nq * chips, chips), pl.ds(0, t), cols(c)], sib
        elif k == 1:
            src, dst, dev = acc1.at[ochip, pl.ds(0, half), cols(c)], h1buf.at[c, 0], right
        elif k == 2:
            src, dst, dev = acc1.at[ochip, pl.ds(half, half), cols(c)], h1buf.at[c, 1], left
        elif k == 3:
            src, dst, dev = acc1.at[rchip, pl.ds(0, t), cols(c)], h2buf.at[c, 0], right
        else:
            src, dst, dev = acc1.at[lchip, pl.ds(0, t), cols(c)], h2buf.at[c, 1], left
        return send(src, dst, r_send.at[c, k], r_recv.at[c, k], dev)

    def out_cols(c):
        def step(e, _):
            n = c * g_loc + e
            w2copy(n).wait()
            o = jnp.dot(ubuf[e], w2buf[lax.rem(n, nw2)], preferred_element_type=F32)
            ebuf[e] = o.astype(BF16).astype(F32)

            @pl.when(n + nw2 < n2 * g_loc)
            def _():
                w2copy(n + nw2).start()

            return 0

        lax.fori_loop(0, g_loc, step, 0)

        def comb(s, _):
            at = pl.ds(pl.multiple_of(s * cp, cp), cp)
            es = jnp.concatenate([ebuf[e, at] for e in range(g_loc)], axis=0).astype(BF16)
            p = jnp.dot(gbuf[s], es, preferred_element_type=F32)
            place = s // 2 + jnp.where(lax.rem(s, 2) == core, 0, chips)
            acc1[place, pl.ds(0, t), cols(c)] = p[:t] + p[t:2 * t] + p[2 * t:]
            return 0

        lax.fori_loop(0, ep, comb, 0)

    def stage_b(c):
        rcopy(c, 0).wait_recv()

        def add(j, _):
            acc1[j, pl.ds(0, t), cols(c)] += acc3[c // nq * chips + j, pl.ds(0, t), cols(c)]
            return 0

        lax.fori_loop(0, chips, add, 0)
        rcopy(c, 1).start()
        rcopy(c, 2).start()

    def stage_c(c):
        rcopy(c, 1).wait_recv()
        acc1[rchip, pl.ds(0, half), cols(c)] += h1buf[c, 0]
        rcopy(c, 3).start()
        rcopy(c, 2).wait_recv()
        acc1[lchip, pl.ds(half, half), cols(c)] += h1buf[c, 1]
        rcopy(c, 4).start()

    def stage_d(c):
        rcopy(c, 3).wait_recv()
        rcopy(c, 4).wait_recv()
        moe = acc1[chip, pl.ds(0, t), cols(c)] + h2buf[c, 0] + h2buf[c, 1]
        at = pl.ds(pl.multiple_of(c * ncol, ncol), ncol)
        y_ref[:, at] = (h_ref[:, at].astype(F32) + moe).astype(BF16)
        for k in range(5):
            rcopy(c, k).wait_send()

    def tail_step(i, _):
        @pl.when(i < n2)
        def _():
            out_cols(i)

            @pl.when(i == 0)
            def _():
                pl.semaphore_wait(ready, 1)

            rcopy(i, 0).start()

        @pl.when((i >= 1) & (i - 1 < n2))
        def _():
            stage_b(i - 1)

        @pl.when((i >= 2) & (i - 2 < n2))
        def _():
            stage_c(i - 2)

        @pl.when(i >= 3)
        def _():
            stage_d(i - 3)

        return 0

    lax.fori_loop(0, n2 + 3, tail_step, 0)
    for k in range(7):
        mcopy(k).wait_send()

    def drain(c, _):
        for k in range(8):
            zcopy(c, k).wait_send()
        return 0

    lax.fori_loop(0, nz, drain, 0)


def moe(ep, meta, z, h, w1, w3, w2, cap, ncol):
    nz, t, kc = z.shape
    g_loc, d, ff = w1.shape
    cp = -(-cap // 8) * 8
    rows = ep * cp
    n2 = d // ncol
    vm = lambda *s: pltpu.VMEM(s, BF16)
    vf = lambda *s: pltpu.VMEM(s, F32)
    hbm = pl.BlockSpec(memory_space=pltpu.HBM)
    vmem = pl.BlockSpec(memory_space=pltpu.VMEM)
    dma = pltpu.SemaphoreType.DMA
    return pl.pallas_call(
        functools.partial(moe_kernel, ep, (g_loc, cp, ncol)),
        in_specs=[hbm, hbm, vmem, hbm, hbm, hbm],
        out_specs=vmem,
        out_shape=jax.ShapeDtypeStruct((t, d), BF16),
        scratch_shapes=[
            vf(ep, *meta.shape), vm(nz, ep, t, kc), vm(ep, g_loc * cp, t), vm(ep, 3 * t, g_loc * cp),
            vm(NW, 2, kc, ff), vf(g_loc, rows, ff), vf(g_loc, rows, ff), vm(g_loc, rows, kc), vm(g_loc, rows, ff),
            vm(NW2, ff, ncol), vf(g_loc, rows, ncol), vf(n2, 2, t // 2, ncol), vf(n2, 2, t, ncol),
            dma((2,)), dma((7,)), dma((7,)), dma((nz, 8)), dma((nz, 8)), dma((NW, 2)), dma((NW2,)),
            dma((n2, 5)), dma((n2, 5)), pltpu.SemaphoreType.REGULAR,
        ],
        compiler_params=pltpu.CompilerParams(collective_id=0, has_side_effects=True, vmem_limit_bytes=67043328),
        cost_estimate=pl.CostEstimate(flops=6 * g_loc * rows * d * ff, bytes_accessed=6 * g_loc * d * ff, transcendentals=0),
        name="moe",
    )(meta, z, h, w1, w3, w2)


def solution(mesh):
    ep = mesh.shape['ep']
    tok = P(('dp', 'ep'))
    rep = P()
    exs = P('ep')

    def body(x, idx, gates, g1, wq, wk, wv, wo, g2, w1, w3, w2):
        n, s_len, d = x.shape
        t = n * s_len
        top = idx.shape[-1]
        avg = top * t // (w1.shape[0] * ep)
        cap = avg + avg // 2
        h, z = attention(x.reshape(t, d), g1, g2, wq, wk, wv, wo, s_len, NZ)
        pad = ((0, 0), (0, -t % 128))
        meta = jnp.concatenate([jnp.pad(idx.reshape(t, top).T.astype(F32), pad, constant_values=-1.0),
                                jnp.pad(gates.reshape(t, top).T, pad)], axis=0)
        return moe(ep, meta, z, h, w1, w3, w2, cap, NCOL).reshape(n, s_len, d)

    return jax.shard_map(body, mesh=mesh, in_specs=(tok, tok, tok, rep, rep, rep, rep, rep, rep, exs, exs, exs), out_specs=tok, check_vma=False)
```

time: 343 us -> 165 us (0.48); the launches traced: 339 us -> 165 us
  Pallas kernels: 20.4 us -> 156 us
  matrix products: 122 us -> 0 us
  waiting for transfers between devices: 78 us -> 0 us
  local copies, waits for them, and re-layouts: 53.5 us -> 7.27 us
  other arithmetic: 26.6 us -> 1.32 us
  blocking collectives: 24.9 us -> 0 us
  between operations: 13.8 us -> 0.03 us
    pallas_call x0 -> x1, Pallas kernels: none -> 137 us  [moe(): pl.pallas_call(functools.partial(moe_kernel, ep, (g_loc, cp, ncol)), in_s...]
    dot_general x6 -> x0, matrix products: 122 us -> none  [the longest x1 38.2 us: body(): h1 = jnp.einsum('gnd,gdf->gnf', r, w1, preferred_element_type=F32)]
    reduce_scatter x1 -> x0, waiting for transfers between devices: 68.7 us -> none  [body(): moe = lax.psum_scatter(part, 'ep', scatter_dimension=0)]
    convert_element_type x4 -> x2, local copies, waits for them, and re-layouts: 25.4 us -> 0.09 us  [body(): idx.reshape(t, top).T.astype(F32)]
    transpose x2 -> x0, local copies, waits for them, and re-layouts: 25 us -> none  [the longest x1 12.5 us: body(): r.reshape(ep, g_loc, cap, d).transpose(1, 0, 2, 3)]
    all_gather x1 -> x0, blocking collectives: 24.9 us -> none  [body(): meta = lax.all_gather(meta, 'ep')]
    reduce_sum x2 -> x0, other arithmetic: 19.3 us -> none  [the longest x1 19.2 us: body(): part = part.reshape(ep, 3, t, d).sum(axis=1)]
    all_gather x1 -> x0, waiting for transfers between devices: 9.28 us -> none  [body(): zs = lax.all_gather(z, 'ep')]
  transfers between devices with their start and end apart: 2 -> 0, of which waited for: 2 -> 0; matrix products, arithmetic and copies ran while one was open for 2% -> 0% of each run, Pallas kernels for 0% -> 0%
where the time goes in v2:
time: 165 us
  Pallas kernels  156 us (95%)
  local copies, waits for them, and re-layouts  7.27 us (4%)
    pallas_call x1, Pallas kernels, moe(): pl.pallas_call(functools.partial(moe_kernel, ep, (g_loc, cp, ncol)), in_s...  137 us
    pallas_call x1, Pallas kernels, attention(): pl.pallas_call(functools.partial(attn_kernel, hb, seq), grid=(wid // c,),...  19.5 us
    unnamed x12, local copies, waits for them, and re-layouts  7.09 us

profile of v2, /device:TPU:112, one launch (start us, length us, event | category | flops | bytes accessed | tf_op | source)
XLA Modules:
  0.0 165.1 jit_solution(13380044056660232116)
XLA Ops:
  0.0 0.7 convert_element_type.11
  0.7 0.1 convert_element_type.12
  0.8 0.7 copy.16
  1.5 0.1 reshape.17
  1.6 0.6 select_maximum_fusion.meta_ref
  2.2 0.0 copy-start
  2.2 1.1 copy-done
  3.3 0.0 copy-start.1
  3.3 0.7 copy-done.1
  4.0 0.0 copy-start.2
  4.0 0.7 copy-done.2
  4.7 19.5 %attention.1 = (bf16[192,2048]{1,0:T(8,128)(2,1)S(1)}, bf16[4,192,512]{2,1,0:T(8,128)(2,1)S(1)}) custom-call(bf16[192,2048]{1,0:T(8,128)(2,1)S(1)} %bitcast.10, f32[1,2048]{1,0:T(1,128)S(1)} %bitcast.11, f32[1,2048]{1,0:T(1,128)S(1)} %bitcast.12, bf16[2048,2048]{1,0:T(8,128)(2,1)} %wq_ref.1, bf16[2048,2048]{1,0:T(8,128)(2,1)} %wk_ref.1, ...), custom_call_target="tpu_custom_call" | custom-call | flops 6442450944 | bytes 33554432 | tf_op jit(solution)/shard_map/attention/pallas_call | solution.py:61
  24.3 0.0 copy-start.3
  24.3 0.9 copy-done.3
  25.2 0.0 copy-start.4
  25.2 0.9 copy-done.4
  26.1 136.9 %moe.1 = bf16[192,2048]{1,0:T(8,128)(2,1)} custom-call(f32[16,256]{1,0:T(8,128)} %select_maximum_fusion.meta_ref, bf16[4,192,512]{2,1,0:T(8,128)(2,1)} %copy-done.4, bf16[192,2048]{1,0:T(8,128)(2,1)} %copy-done.3, bf16[8,2048,1024]{2,1,0:T(8,128)(2,1)} %w1_ref.1, bf16[8,2048,1024]{2,1,0:T(8,128)(2,1)} %w3_ref.1, bf16[8,1024,2048]{2,1,0:T(8,128)(2,1)} %w2_ref.1), custom_call_target="tpu_custom_call" | custom-call | flops 32212254720 | bytes 100663296 | tf_op jit(solution)/shard_map/moe/pallas_call | solution.py:407
  163.0 2.1 %copy.18 = bf16[3,64,2048]{2,1,0:T(8,128)(2,1)} copy(bf16[3,64,2048]{2,1,0:T(8,128)(2,1)} %bitcast.13) | data formatting | bytes 1572864
  (1 shorter events, 0.0 us)
Async XLA Ops:
  2.2 1.1 copy-start
  3.3 0.7 copy-start.1
  4.0 0.7 copy-start.2
  24.3 0.9 copy-start.3
  25.2 0.9 copy-start.4

commit v3 on v2

--- a/solution.py
+++ b/solution.py
@@ -16,7 +16,14 @@
     return (xf * lax.rsqrt(jnp.mean(xf * xf, axis=-1, keepdims=True) + EPS) * g).astype(BF16)
 
 
-def attn_kernel(hb, seq, x_ref, g1_ref, g2_ref, wq_ref, wk_ref, wv_ref, wo_ref, h_ref, z_ref, xn_ref, acc_ref):
+def split3(g):
+    hi = g.astype(BF16)
+    r = g - hi.astype(F32)
+    mid = r.astype(BF16)
+    return hi, mid, (r - mid.astype(F32)).astype(BF16)
+
+
+def attn_kernel(hb, seq, x_ref, idx_ref, gate_ref, g1_ref, g2_ref, wq_ref, wk_ref, wv_ref, wo_ref, h_ref, z_ref, meta_ref, xn_ref, acc_ref):
     i = pl.program_id(0)
     t = x_ref.shape[0]
 
@@ -24,6 +31,17 @@
     def _():
         xn_ref[...] = rms(x_ref[...].astype(F32), g1_ref[...])
         acc_ref[...] = jnp.zeros_like(acc_ref)
+        top, tp = meta_ref.shape[0] // 2, meta_ref.shape[1]
+        at, to = lax.broadcasted_iota(jnp.int32, (t, tp), 0), lax.broadcasted_iota(jnp.int32, (t, tp), 1)
+        eye = jnp.where(at == to, 1.0, 0.0).astype(BF16)
+
+        def turn(a):
+            return lax.dot_general(a, eye, (((0,), (0,)), ((), ())), preferred_element_type=F32)
+
+        real = lax.broadcasted_iota(jnp.int32, (top, tp), 1) < t
+        meta_ref[:top] = jnp.where(real, turn(idx_ref[...].astype(F32).astype(BF16)), -1.0)
+        hi, mid, lo = split3(gate_ref[...])
+        meta_ref[top:] = turn(hi) + turn(mid) + turn(lo)
 
     xn = xn_ref[...]
     q = jnp.dot(xn, wq_ref[...], preferred_element_type=F32).astype(BF16)
@@ -54,8 +72,9 @@
             z_ref[c] = z[:, c * kc:(c + 1) * kc]
 
 
-def attention(xf, g1, g2, wq, wk, wv, wo, seq, nz, hb=2):
+def attention(xf, idx, gates, g1, g2, wq, wk, wv, wo, seq, nz, hb):
     t, d = xf.shape
+    top, tp = idx.shape[1], t + -t % 128
     wid = wq.shape[1]
     c = hb * HEAD
     return pl.pallas_call(
@@ -63,6 +82,8 @@
         grid=(wid // c,),
         in_specs=[
             pl.BlockSpec((t, d), lambda i: (0, 0)),
+            pl.BlockSpec((t, top), lambda i: (0, 0)),
+            pl.BlockSpec((t, top), lambda i: (0, 0)),
             pl.BlockSpec((1, d), lambda i: (0, 0)),
             pl.BlockSpec((1, d), lambda i: (0, 0)),
             pl.BlockSpec((d, c), lambda i: (0, i)),
@@ -70,32 +91,38 @@
             pl.BlockSpec((d, c), lambda i: (0, i)),
             pl.BlockSpec((c, d), lambda i: (i, 0)),
         ],
-        out_specs=[pl.BlockSpec((t, d), lambda i: (0, 0)), pl.BlockSpec((nz, t, d // nz), lambda i: (0, 0, 0))],
-        out_shape=[jax.ShapeDtypeStruct((t, d), BF16), jax.ShapeDtypeStruct((nz, t, d // nz), BF16)],
+        out_specs=[pl.BlockSpec((t, d), lambda i: (0, 0)), pl.BlockSpec((nz, t, d // nz), lambda i: (0, 0, 0)),
+                   pl.BlockSpec((2 * top, tp), lambda i: (0, 0))],
+        out_shape=[jax.ShapeDtypeStruct((t, d), BF16), jax.ShapeDtypeStruct((nz, t, d // nz), BF16),
+                   jax.ShapeDtypeStruct((2 * top, tp), F32)],
         scratch_shapes=[pltpu.VMEM((t, d), BF16), pltpu.VMEM((t, d), F32)],
-        compiler_params=pltpu.CompilerParams(dimension_semantics=("arbitrary",), vmem_limit_bytes=48 * 2**20),
+        compiler_params=pltpu.CompilerParams(dimension_semantics=("arbitrary",), vmem_limit_bytes=67043328),
         cost_estimate=pl.CostEstimate(flops=8 * t * d * wid, bytes_accessed=8 * d * wid, transcendentals=0),
         name="attention",
-    )(xf, g1.reshape(1, d), g2.reshape(1, d), wq, wk, wv, wo)
+    )(xf, idx, gates, g1.reshape(1, d), g2.reshape(1, d), wq, wk, wv, wo)
 
 
 MESH = pl.DeviceIdType.MESH
-NZ, NW, NW2, NCOL = 4, 4, 8, 256
-
-
-def moe_kernel(ep, cfg, meta_ref, z_ref, h_ref, w1_ref, w3_ref, w2_ref, y_ref,
-               mbuf, zbuf, dbuf, gbuf, wbuf, acc1, acc3, rbuf, ubuf, w2buf, ebuf, h1buf, h2buf,
-               load_sem, m_send, m_recv, z_send, z_recv, w_sem, w2_sem, r_send, r_recv, ready):
+NZ, NW, NW2, NCOL, HB = 8, 6, 8, 256, 4
+
+
+def moe_kernel(ep, cfg, meta_ref, z_ref, h_hbm, w1_ref, w3_ref, w2_ref, y_ref,
+               mbuf, zbuf, dbuf, gbuf, wbuf, acc1, acc3, rbuf, ubuf, w2buf, h1buf, h2buf, h_ref,
+               load_sem, m_send, m_recv, z_send, z_recv, w_sem, w2_sem, r_send, r_recv, y_sem, ready):
     g_loc, cp, ncol = cfg
     nz, _, t, kc = zbuf.shape
     tp = mbuf.shape[2]
     ff = acc1.shape[2]
     d = nz * kc
+    kw = 2 * kc
+    nk = nz // 2
     rows = ep * cp
     chips = ep // 2
     half = t // 2
     n2 = d // ncol
     nq = ff // ncol
+    fit = (rows - t) // cp
+    assert fit * nq >= ep
     nw, nw2 = wbuf.shape[0], w2buf.shape[0]
 
     me = lax.axis_index('ep')
@@ -111,7 +138,7 @@
         e, c = lax.rem(n, g_loc), n // g_loc
         ref = w3_ref if which else w1_ref
         slot = lax.rem(n, nw)
-        return pltpu.make_async_copy(ref.at[e, pl.ds(c * kc, kc)], wbuf.at[slot, which], w_sem.at[slot, which])
+        return pltpu.make_async_copy(ref.at[e, pl.ds(c * kw, kw)], wbuf.at[slot, which], w_sem.at[slot, which])
 
     def w2copy(n):
         e, c = lax.rem(n, g_loc), n // g_loc
@@ -120,8 +147,10 @@
 
     zload = pltpu.make_async_copy(z_ref, zbuf.at[:, me], load_sem.at[0])
     mload = pltpu.make_async_copy(meta_ref, mbuf.at[me], load_sem.at[1])
+    hload = pltpu.make_async_copy(h_hbm, h_ref, load_sem.at[2])
     zload.start()
     mload.start()
+    hload.start()
     for n in range(nw):
         wcopy(n, 0).start()
         wcopy(n, 1).start()
@@ -168,11 +197,26 @@
         for k in (2, 5, 6, 7):
             zcopy(c, k).wait_recv()
 
+    def hop(m):
+        @pl.when(m < nz)
+        def _():
+            stage1(m)
+
+        @pl.when(m + 2 < nz)
+        def _():
+            own(m + 2)
+
+    def share(m):
+        @pl.when(m < nz)
+        def _():
+            stage2(m)
+
     mload.wait()
     for k in (0, 1, 2):
         mcopy(k).start()
     zload.wait()
     own(0)
+    own(1)
 
     def zero(e, _):
         acc1[e] = jnp.zeros_like(acc1[e])
@@ -185,9 +229,9 @@
     mcopy(4).start()
     mcopy(1).wait_recv()
     mcopy(5).start()
-    own(1)
     mcopy(3).wait_recv()
     mcopy(6).start()
+    hop(0)
     for k in (2, 4, 5, 6):
         mcopy(k).wait_recv()
 
@@ -217,73 +261,83 @@
 
         slots = lax.rem(lax.broadcasted_iota(jnp.int32, (t, g_loc * cp), 1), cp).astype(F32)
         sel = widen(place.astype(BF16)) == slots
-        hi = gate.astype(BF16)
-        r1 = gate - hi.astype(F32)
-        mid = r1.astype(BF16)
-        lo = (r1 - mid.astype(F32)).astype(BF16)
-        for i, part in enumerate((hi, mid, lo)):
+        for i, part in enumerate(split3(gate)):
             gbuf[s, i * t:(i + 1) * t] = jnp.where(sel, widen(part), 0.0).astype(BF16)
         return 0
 
-    stage1(0)
-    lax.fori_loop(0, ep // 2, build, 0)
-    stage2(0)
-    lax.fori_loop(ep // 2, ep, build, 0)
+    quarter = ep // 4
+    lax.fori_loop(0, quarter, build, 0)
+    hop(1)
+    lax.fori_loop(quarter, 2 * quarter, build, 0)
+    share(0)
+    lax.fori_loop(2 * quarter, 3 * quarter, build, 0)
+    hop(2)
+    lax.fori_loop(3 * quarter, ep, build, 0)
+    share(1)
 
     def dispatch(c):
         def pair(p, _):
-            a = jnp.dot(dbuf[2 * p], zbuf[c, 2 * p], preferred_element_type=F32)
-            b = jnp.dot(dbuf[2 * p + 1], zbuf[c, 2 * p + 1], preferred_element_type=F32)
-            for e in range(g_loc):
-                sl = slice(e * cp, (e + 1) * cp)
-                rbuf[e, pl.ds(pl.multiple_of(p * 2 * cp, 2 * cp), 2 * cp)] = jnp.concatenate([a[sl], b[sl]], axis=0).astype(BF16)
+            for q in range(2):
+                a = jnp.dot(dbuf[2 * p], zbuf[2 * c + q, 2 * p], preferred_element_type=F32)
+                b = jnp.dot(dbuf[2 * p + 1], zbuf[2 * c + q, 2 * p + 1], preferred_element_type=F32)
+                for e in range(g_loc):
+                    sl = slice(e * cp, (e + 1) * cp)
+                    rbuf[e, pl.ds(pl.multiple_of(p * 2 * cp, 2 * cp), 2 * cp), q * kc:(q + 1) * kc] = (
+                        jnp.concatenate([a[sl], b[sl]], axis=0).astype(BF16))
             return 0
 
         lax.fori_loop(0, ep // 2, pair, 0)
 
-    def expert_in(c, last):
-        def step(e, _):
-            n = c * g_loc + e
-            slot = lax.rem(n, nw)
-            wcopy(n, 0).wait()
-            wcopy(n, 1).wait()
-            r = rbuf[e]
-            a = acc1[e] + jnp.dot(r, wbuf[slot, 0], preferred_element_type=F32)
-            b = acc3[e] + jnp.dot(r, wbuf[slot, 1], preferred_element_type=F32)
-            if last:
-                ubuf[e] = (a / (1.0 + jnp.exp(-a)) * b).astype(BF16)
-            else:
-                acc1[e] = a
-                acc3[e] = b
-
-            @pl.when(n + nw < nz * g_loc)
+    def experts_in(c, last):
+        def step(i, _):
+            n = c * g_loc + 2 * i
+            for q in range(2):
+                wcopy(n + q, 0).wait()
+                wcopy(n + q, 1).wait()
+            for q in range(2):
+                e, slot = 2 * i + q, lax.rem(n + q, nw)
+                r = rbuf[e]
+                a = acc1[e] + jnp.dot(r, wbuf[slot, 0], preferred_element_type=F32)
+                b = acc3[e] + jnp.dot(r, wbuf[slot, 1], preferred_element_type=F32)
+                if last:
+                    ubuf[e] = (a / (1.0 + jnp.exp(-a)) * b).astype(BF16)
+                else:
+                    acc1[e] = a
+                    acc3[e] = b
+
+            @pl.when(n + nw < nk * g_loc)
             def _():
-                wcopy(n + nw, 0).start()
-                wcopy(n + nw, 1).start()
+                for q in range(2):
+                    wcopy(n + q + nw, 0).start()
+                    wcopy(n + q + nw, 1).start()
 
             return 0
 
         return step
 
     def chunk(c, _):
-        stage3(c)
+        stage3(2 * c)
+        stage3(2 * c + 1)
         dispatch(c)
-
-        @pl.when(c + 2 < nz)
-        def _():
-            own(c + 2)
-
-        stage1(c + 1)
-        step = expert_in(c, False)
-        lax.fori_loop(0, g_loc // 2, step, 0)
-        stage2(c + 1)
-        lax.fori_loop(g_loc // 2, g_loc, step, 0)
+        step = experts_in(c, False)
+
+        def portion(i, _):
+            @pl.when(i > 0)
+            def _():
+                hop(2 * c + 2 + i)
+                share(2 * c + 1 + i)
+
+            return lax.fori_loop(i * 2 - jnp.minimum(i, 1), jnp.minimum(i * 2 + 1, g_loc // 2), step, 0)
+
+        lax.fori_loop(0, 3, portion, 0)
         return 0
 
-    lax.fori_loop(0, nz - 1, chunk, 0)
+    lax.fori_loop(0, nk - 1, chunk, 0)
+    stage3(nz - 2)
     stage3(nz - 1)
-    dispatch(nz - 1)
-    lax.fori_loop(0, g_loc, expert_in(nz - 1, True), 0)
+    dispatch(nk - 1)
+    lax.fori_loop(0, g_loc // 2, experts_in(nk - 1, True), 0)
+    hload.wait()
     pl.semaphore_signal(ready, inc=1, device_id={'ep': sib}, device_id_type=MESH)
 
     def cols(c):
@@ -304,29 +358,37 @@
         return send(src, dst, r_send.at[c, k], r_recv.at[c, k], dev)
 
     def out_cols(c):
-        def step(e, _):
-            n = c * g_loc + e
-            w2copy(n).wait()
-            o = jnp.dot(ubuf[e], w2buf[lax.rem(n, nw2)], preferred_element_type=F32)
-            ebuf[e] = o.astype(BF16).astype(F32)
+        def step(i, _):
+            n = c * g_loc + 4 * i
+            for q in range(4):
+                w2copy(n + q).wait()
+            for q in range(4):
+                e = 4 * i + q
+                o = jnp.dot(ubuf[e], w2buf[lax.rem(n + q, nw2)], preferred_element_type=F32)
+                o = o.astype(BF16).astype(F32)
+                for r in range(ep):
+                    acc3[e, t + r % fit * cp:t + (r % fit + 1) * cp, r // fit * ncol:(r // fit + 1) * ncol] = o[r * cp:(r + 1) * cp]
 
             @pl.when(n + nw2 < n2 * g_loc)
             def _():
-                w2copy(n + nw2).start()
+                for q in range(4):
+                    w2copy(n + q + nw2).start()
 
             return 0
 
-        lax.fori_loop(0, g_loc, step, 0)
-
-        def comb(s, _):
-            at = pl.ds(pl.multiple_of(s * cp, cp), cp)
-            es = jnp.concatenate([ebuf[e, at] for e in range(g_loc)], axis=0).astype(BF16)
-            p = jnp.dot(gbuf[s], es, preferred_element_type=F32)
-            place = s // 2 + jnp.where(lax.rem(s, 2) == core, 0, chips)
-            acc1[place, pl.ds(0, t), cols(c)] = p[:t] + p[t:2 * t] + p[2 * t:]
+        lax.fori_loop(0, g_loc // 4, step, 0)
+
+        def comb(i, _):
+            for q in range(4):
+                s = 4 * i + q
+                at = pl.ds(pl.multiple_of(t + lax.rem(s, fit) * cp, 8), cp), pl.ds(pl.multiple_of(s // fit * ncol, ncol), ncol)
+                es = jnp.concatenate([acc3[e, at[0], at[1]] for e in range(g_loc)], axis=0).astype(BF16)
+                p = jnp.dot(gbuf[s], es, preferred_element_type=F32)
+                place = s // 2 + jnp.where(q % 2 == core, 0, chips)
+                acc1[place, pl.ds(0, t), cols(c)] = p[:t] + p[t:2 * t] + p[2 * t:]
             return 0
 
-        lax.fori_loop(0, ep, comb, 0)
+        lax.fori_loop(0, ep // 4, comb, 0)
 
     def stage_b(c):
         rcopy(c, 0).wait_recv()
@@ -347,12 +409,17 @@
         acc1[lchip, pl.ds(half, half), cols(c)] += h1buf[c, 1]
         rcopy(c, 4).start()
 
+    def ycopy(c):
+        at = pl.ds(pl.multiple_of(c * ncol, ncol), ncol)
+        return pltpu.make_async_copy(h_ref.at[:, at], y_ref.at[:, at], y_sem.at[c])
+
     def stage_d(c):
         rcopy(c, 3).wait_recv()
         rcopy(c, 4).wait_recv()
         moe = acc1[chip, pl.ds(0, t), cols(c)] + h2buf[c, 0] + h2buf[c, 1]
         at = pl.ds(pl.multiple_of(c * ncol, ncol), ncol)
-        y_ref[:, at] = (h_ref[:, at].astype(F32) + moe).astype(BF16)
+        h_ref[:, at] = (h_ref[:, at].astype(F32) + moe).astype(BF16)
+        ycopy(c).start()
         for k in range(5):
             rcopy(c, k).wait_send()
 
@@ -391,6 +458,12 @@
         return 0
 
     lax.fori_loop(0, nz, drain, 0)
+
+    def finish(c, _):
+        ycopy(c).wait()
+        return 0
+
+    lax.fori_loop(0, n2, finish, 0)
 
 
 def moe(ep, meta, z, h, w1, w3, w2, cap, ncol):
@@ -402,19 +475,18 @@
     vm = lambda *s: pltpu.VMEM(s, BF16)
     vf = lambda *s: pltpu.VMEM(s, F32)
     hbm = pl.BlockSpec(memory_space=pltpu.HBM)
-    vmem = pl.BlockSpec(memory_space=pltpu.VMEM)
     dma = pltpu.SemaphoreType.DMA
     return pl.pallas_call(
         functools.partial(moe_kernel, ep, (g_loc, cp, ncol)),
-        in_specs=[hbm, hbm, vmem, hbm, hbm, hbm],
-        out_specs=vmem,
+        in_specs=[hbm] * 6,
+        out_specs=hbm,
         out_shape=jax.ShapeDtypeStruct((t, d), BF16),
         scratch_shapes=[
             vf(ep, *meta.shape), vm(nz, ep, t, kc), vm(ep, g_loc * cp, t), vm(ep, 3 * t, g_loc * cp),
-            vm(NW, 2, kc, ff), vf(g_loc, rows, ff), vf(g_loc, rows, ff), vm(g_loc, rows, kc), vm(g_loc, rows, ff),
-            vm(NW2, ff, ncol), vf(g_loc, rows, ncol), vf(n2, 2, t // 2, ncol), vf(n2, 2, t, ncol),
-            dma((2,)), dma((7,)), dma((7,)), dma((nz, 8)), dma((nz, 8)), dma((NW, 2)), dma((NW2,)),
-            dma((n2, 5)), dma((n2, 5)), pltpu.SemaphoreType.REGULAR,
+            vm(NW, 2, 2 * kc, ff), vf(g_loc, rows, ff), vf(g_loc, rows, ff), vm(g_loc, rows, 2 * kc), vm(g_loc, rows, ff),
+            vm(NW2, ff, ncol), vf(n2, 2, t // 2, ncol), vf(n2, 2, t, ncol), vm(t, d),
+            dma((3,)), dma((7,)), dma((7,)), dma((nz, 8)), dma((nz, 8)), dma((NW, 2)), dma((NW2,)),
+            dma((n2, 5)), dma((n2, 5)), dma((n2,)), pltpu.SemaphoreType.REGULAR,
         ],
         compiler_params=pltpu.CompilerParams(collective_id=0, has_side_effects=True, vmem_limit_bytes=67043328),
         cost_estimate=pl.CostEstimate(flops=6 * g_loc * rows * d * ff, bytes_accessed=6 * g_loc * d * ff, transcendentals=0),
@@ -434,10 +506,7 @@
         top = idx.shape[-1]
         avg = top * t // (w1.shape[0] * ep)
         cap = avg + avg // 2
-        h, z = attention(x.reshape(t, d), g1, g2, wq, wk, wv, wo, s_len, NZ)
-        pad = ((0, 0), (0, -t % 128))
-        meta = jnp.concatenate([jnp.pad(idx.reshape(t, top).T.astype(F32), pad, constant_values=-1.0),
-                                jnp.pad(gates.reshape(t, top).T, pad)], axis=0)
+        h, z, meta = attention(x.reshape(t, d), idx.reshape(t, top), gates.reshape(t, top), g1, g2, wq, wk, wv, wo, s_len, NZ, HB)
         return moe(ep, meta, z, h, w1, w3, w2, cap, NCOL).reshape(n, s_len, d)
 
     return jax.shard_map(body, mesh=mesh, in_specs=(tok, tok, tok, rep, rep, rep, rep, rep, rep, exs, exs, exs), out_specs=tok, check_vma=False)

time: 165 us -> 142 us (0.86)
  Pallas kernels: 156 us -> 137 us
  local copies, waits for them, and re-layouts: 7.27 us -> 4.98 us
    pallas_call x1, Pallas kernels: 137 us -> 120 us  [moe(): pl.pallas_call(functools.partial(moe_kernel, ep, (g_loc, cp, ncol)), in_s...]
    unnamed x12 -> x3, local copies, waits for them, and re-layouts: 7.09 us -> 4.98 us
    pallas_call x1, Pallas kernels: 19.5 us -> 17.5 us  [attention(): pl.pallas_call(functools.partial(attn_kernel, hb, seq), grid=(wid // c,),...]
where the time goes in v3:
time: 142 us
  Pallas kernels  137 us (96%)
  local copies, waits for them, and re-layouts  4.98 us (4%)
    pallas_call x1, Pallas kernels, moe(): pl.pallas_call(functools.partial(moe_kernel, ep, (g_loc, cp, ncol)), in_s...  120 us
    pallas_call x1, Pallas kernels, attention(): pl.pallas_call(functools.partial(attn_kernel, hb, seq), grid=(wid // c,),...  17.5 us
    unnamed x3, local copies, waits for them, and re-layouts  4.98 us

profile of v3, /device:TPU:112, one launch (start us, length us, event | category | flops | bytes accessed | tf_op | source)
XLA Modules:
  0.0 142.0 jit_solution(9712844424049013135)
XLA Ops:
  0.0 1.4 %copy.13 = s32[3,64,8]{2,1,0:T(8,128)} copy(s32[3,64,8]{1,2,0:T(8,128)} %param.13) | data formatting | bytes 12288 | tf_op args[1]
  1.4 1.4 %copy.14 = f32[3,64,8]{2,1,0:T(8,128)} copy(f32[3,64,8]{1,2,0:T(8,128)} %param.14) | data formatting | bytes 12288 | tf_op args[2]
  2.9 17.5 %attention.1 = (bf16[192,2048]{1,0:T(8,128)(2,1)}, bf16[8,192,256]{2,1,0:T(8,128)(2,1)}, f32[16,256]{1,0:T(8,128)}) custom-call(bf16[192,2048]{1,0:T(8,128)(2,1)} %bitcast.7, s32[192,8]{1,0:T(8,128)} %bitcast.8, f32[192,8]{1,0:T(8,128)} %bitcast.9, f32[1,2048]{1,0:T(1,128)} %bitcast.10, f32[1,2048]{1,0:T(1,128)} %bitcast.11, bf16[2048,2048]{1,0:T(8,128)(2,1)} %wq_ref.1, ...), custom_call_target="tpu_custom_call" | custom-call | flops 6442450944 | bytes 33554432 | tf_op jit(solution)/shard_map/attention/pallas_call | solution.py:80
  20.4 119.6 %moe.1 = bf16[192,2048]{1,0:T(8,128)(2,1)} custom-call(f32[16,256]{1,0:T(8,128)} %get-tuple-element.8.meta_ref, bf16[8,192,256]{2,1,0:T(8,128)(2,1)} %get-tuple-element.9.z_ref, bf16[192,2048]{1,0:T(8,128)(2,1)} %get-tuple-element.10.h_hbm, bf16[8,2048,1024]{2,1,0:T(8,128)(2,1)} %w1_ref.1, bf16[8,2048,1024]{2,1,0:T(8,128)(2,1)} %w3_ref.1, ...), custom_call_target="tpu_custom_call" | custom-call | flops 32212254720 | bytes 100663296 | tf_op jit(solution)/shard_map/moe/pallas_call | solution.py:479
  139.9 2.1 %copy.16 = bf16[3,64,2048]{2,1,0:T(8,128)(2,1)} copy(bf16[3,64,2048]{2,1,0:T(8,128)(2,1)} %bitcast.6) | data formatting | bytes 1572864

commit v4 on v3

--- a/solution.py
+++ b/solution.py
@@ -32,16 +32,15 @@
         xn_ref[...] = rms(x_ref[...].astype(F32), g1_ref[...])
         acc_ref[...] = jnp.zeros_like(acc_ref)
         top, tp = meta_ref.shape[0] // 2, meta_ref.shape[1]
-        at, to = lax.broadcasted_iota(jnp.int32, (t, tp), 0), lax.broadcasted_iota(jnp.int32, (t, tp), 1)
-        eye = jnp.where(at == to, 1.0, 0.0).astype(BF16)
-
-        def turn(a):
-            return lax.dot_general(a, eye, (((0,), (0,)), ((), ())), preferred_element_type=F32)
-
-        real = lax.broadcasted_iota(jnp.int32, (top, tp), 1) < t
-        meta_ref[:top] = jnp.where(real, turn(idx_ref[...].astype(F32).astype(BF16)), -1.0)
-        hi, mid, lo = split3(gate_ref[...])
-        meta_ref[top:] = turn(hi) + turn(mid) + turn(lo)
+        ids, gts = jnp.zeros((top, tp), F32), jnp.zeros((top, tp), F32)
+        for n in range(t // seq):
+            at, to = lax.broadcasted_iota(jnp.int32, (seq, tp), 0), lax.broadcasted_iota(jnp.int32, (seq, tp), 1)
+            move = jnp.where(at + n * seq == to, 1.0, 0.0).astype(BF16)
+            ids += jnp.dot(idx_ref[n].astype(F32).astype(BF16), move, preferred_element_type=F32)
+            hi, mid, lo = [jnp.dot(p, move, preferred_element_type=F32) for p in split3(gate_ref[n])]
+            gts += hi + mid + lo
+        meta_ref[:top] = jnp.where(lax.broadcasted_iota(jnp.int32, (top, tp), 1) < t, ids, -1.0)
+        meta_ref[top:] = gts
 
     xn = xn_ref[...]
     q = jnp.dot(xn, wq_ref[...], preferred_element_type=F32).astype(BF16)
@@ -74,7 +73,8 @@
 
 def attention(xf, idx, gates, g1, g2, wq, wk, wv, wo, seq, nz, hb):
     t, d = xf.shape
-    top, tp = idx.shape[1], t + -t % 128
+    n, top, _ = idx.shape
+    tp = t + -t % 128
     wid = wq.shape[1]
     c = hb * HEAD
     return pl.pallas_call(
@@ -82,8 +82,8 @@
         grid=(wid // c,),
         in_specs=[
             pl.BlockSpec((t, d), lambda i: (0, 0)),
-            pl.BlockSpec((t, top), lambda i: (0, 0)),
-            pl.BlockSpec((t, top), lambda i: (0, 0)),
+            pl.BlockSpec((n, top, seq), lambda i: (0, 0, 0)),
+            pl.BlockSpec((n, top, seq), lambda i: (0, 0, 0)),
             pl.BlockSpec((1, d), lambda i: (0, 0)),
             pl.BlockSpec((1, d), lambda i: (0, 0)),
             pl.BlockSpec((d, c), lambda i: (0, i)),
@@ -134,11 +134,24 @@
         return pltpu.make_async_remote_copy(src_ref=src, dst_ref=dst, send_sem=ssem, recv_sem=rsem,
                                             device_id={'ep': dev}, device_id_type=MESH)
 
-    def wcopy(n, which):
+    def wcopy(n, which, unit):
         e, c = lax.rem(n, g_loc), n // g_loc
         ref = w3_ref if which else w1_ref
         slot = lax.rem(n, nw)
-        return pltpu.make_async_copy(ref.at[e, pl.ds(c * kw, kw)], wbuf.at[slot, which], w_sem.at[slot, which])
+        row = pl.multiple_of((jnp.maximum(2 * c - 1, 0) + unit) * kc, kc)
+        return pltpu.make_async_copy(ref.at[e, pl.ds(row, kc)], wbuf.at[slot, which, unit * kc:(unit + 1) * kc],
+                                     w_sem.at[slot, which, unit])
+
+    def wstart(n):
+        @pl.when(n < (nk + 1) * g_loc)
+        def _():
+            wcopy(n, 0, 0).start()
+            wcopy(n, 1, 0).start()
+
+        @pl.when((n >= g_loc) & (n < nk * g_loc))
+        def _():
+            wcopy(n, 0, 1).start()
+            wcopy(n, 1, 1).start()
 
     def w2copy(n):
         e, c = lax.rem(n, g_loc), n // g_loc
@@ -152,19 +165,18 @@
     mload.start()
     hload.start()
     for n in range(nw):
-        wcopy(n, 0).start()
-        wcopy(n, 1).start()
+        wstart(n)
     for n in range(nw2):
         w2copy(n).start()
 
     barrier = pltpu.get_barrier_semaphore()
-    for dev in (right, left, sib):
-        pl.semaphore_signal(barrier, inc=1, device_id={'ep': dev}, device_id_type=MESH)
-    pl.semaphore_wait(barrier, 3)
+    for k in range(1, ep):
+        pl.semaphore_signal(barrier, inc=1, device_id={'ep': lax.rem(me + k, ep)}, device_id_type=MESH)
+    mload.wait()
+    pl.semaphore_wait(barrier, ep - 1)
 
     def mcopy(k):
-        who, dev = ((me, right), (me, left), (me, sib), (left, right), (left, sib), (right, sib), (opp, sib))[k]
-        return send(mbuf.at[who], mbuf.at[who], m_send.at[k], m_recv.at[k], dev)
+        return send(mbuf.at[me], mbuf.at[me], m_send.at[k - 1], m_recv.at[k - 1], lax.rem(me + k, ep))
 
     def zcopy(c, k):
         if k == 3:
@@ -211,33 +223,17 @@
         def _():
             stage2(m)
 
-    mload.wait()
-    for k in (0, 1, 2):
+    for k in range(1, ep):
         mcopy(k).start()
     zload.wait()
     own(0)
     own(1)
-
-    def zero(e, _):
-        acc1[e] = jnp.zeros_like(acc1[e])
-        acc3[e] = jnp.zeros_like(acc3[e])
-        return 0
-
-    lax.fori_loop(0, g_loc, zero, 0)
-    mcopy(0).wait_recv()
-    mcopy(3).start()
-    mcopy(4).start()
-    mcopy(1).wait_recv()
-    mcopy(5).start()
-    mcopy(3).wait_recv()
-    mcopy(6).start()
-    hop(0)
-    for k in (2, 4, 5, 6):
+    for k in range(1, ep):
         mcopy(k).wait_recv()
 
     base = (me * g_loc).astype(F32)
 
-    def build(s, _):
+    def build(s):
         m = mbuf[s]
         top = m.shape[0] // 2
         ids, gt = m[:top], m[top:]
@@ -263,80 +259,91 @@
         sel = widen(place.astype(BF16)) == slots
         for i, part in enumerate(split3(gate)):
             gbuf[s, i * t:(i + 1) * t] = jnp.where(sel, widen(part), 0.0).astype(BF16)
+
+    def builds(i, _):
+        hop(i)
+        for q in range(4):
+            build(4 * i + q)
         return 0
 
-    quarter = ep // 4
-    lax.fori_loop(0, quarter, build, 0)
-    hop(1)
-    lax.fori_loop(quarter, 2 * quarter, build, 0)
+    lax.fori_loop(0, ep // 4, builds, 0)
     share(0)
-    lax.fori_loop(2 * quarter, 3 * quarter, build, 0)
-    hop(2)
-    lax.fori_loop(3 * quarter, ep, build, 0)
-    share(1)
-
-    def dispatch(c):
-        def pair(p, _):
-            for q in range(2):
-                a = jnp.dot(dbuf[2 * p], zbuf[2 * c + q, 2 * p], preferred_element_type=F32)
-                b = jnp.dot(dbuf[2 * p + 1], zbuf[2 * c + q, 2 * p + 1], preferred_element_type=F32)
-                for e in range(g_loc):
-                    sl = slice(e * cp, (e + 1) * cp)
-                    rbuf[e, pl.ds(pl.multiple_of(p * 2 * cp, 2 * cp), 2 * cp), q * kc:(q + 1) * kc] = (
-                        jnp.concatenate([a[sl], b[sl]], axis=0).astype(BF16))
-            return 0
-
-        lax.fori_loop(0, ep // 2, pair, 0)
-
-    def experts_in(c, last):
+
+    def dispatch(m, q):
+        stage3(m)
+        at = pl.ds(pl.multiple_of(q * kc, kc), kc)
+        for p in range(ep // 2):
+            a = jnp.dot(dbuf[2 * p], zbuf[m, 2 * p], preferred_element_type=F32)
+            b = jnp.dot(dbuf[2 * p + 1], zbuf[m, 2 * p + 1], preferred_element_type=F32)
+            for e in range(g_loc):
+                sl = slice(e * cp, (e + 1) * cp)
+                rbuf[e, p * 2 * cp:(p + 1) * 2 * cp, at] = jnp.concatenate([a[sl], b[sl]], axis=0).astype(BF16)
+
+    def experts_in(c, kind):
+        units = 2 if kind == 'mid' else 1
+        k = units * kc
+
         def step(i, _):
             n = c * g_loc + 2 * i
             for q in range(2):
-                wcopy(n + q, 0).wait()
-                wcopy(n + q, 1).wait()
+                for u in range(units):
+                    wcopy(n + q, 0, u).wait()
+                    wcopy(n + q, 1, u).wait()
             for q in range(2):
                 e, slot = 2 * i + q, lax.rem(n + q, nw)
-                r = rbuf[e]
-                a = acc1[e] + jnp.dot(r, wbuf[slot, 0], preferred_element_type=F32)
-                b = acc3[e] + jnp.dot(r, wbuf[slot, 1], preferred_element_type=F32)
-                if last:
+                r = rbuf[e, :, :k]
+                a = jnp.dot(r, wbuf[slot, 0, :k], preferred_element_type=F32)
+                b = jnp.dot(r, wbuf[slot, 1, :k], preferred_element_type=F32)
+                if kind != 'first':
+                    a = acc1[e] + a
+                    b = acc3[e] + b
+                if kind == 'last':
                     ubuf[e] = (a / (1.0 + jnp.exp(-a)) * b).astype(BF16)
                 else:
                     acc1[e] = a
                     acc3[e] = b
-
-            @pl.when(n + nw < nk * g_loc)
-            def _():
-                for q in range(2):
-                    wcopy(n + q + nw, 0).start()
-                    wcopy(n + q + nw, 1).start()
-
+            wstart(n + nw)
+            wstart(n + nw + 1)
             return 0
 
         return step
 
+    dispatch(0, 0)
+
+    def opening(i, _):
+        @pl.when(i > 0)
+        def _():
+            hop(2)
+            share(1)
+
+        return lax.fori_loop(i * 2, i * 2 + 2, experts_in(0, 'first'), 0)
+
+    lax.fori_loop(0, g_loc // 4, opening, 0)
+    hop(3)
+    share(2)
+
     def chunk(c, _):
-        stage3(2 * c)
-        stage3(2 * c + 1)
-        dispatch(c)
-        step = experts_in(c, False)
+        def pick(q, _):
+            dispatch(2 * c - 1 + q, q)
+            return 0
+
+        lax.fori_loop(0, 2, pick, 0)
+        step = experts_in(c, 'mid')
 
         def portion(i, _):
             @pl.when(i > 0)
             def _():
-                hop(2 * c + 2 + i)
-                share(2 * c + 1 + i)
+                hop(2 * c + 1 + i)
+                share(2 * c + i)
 
             return lax.fori_loop(i * 2 - jnp.minimum(i, 1), jnp.minimum(i * 2 + 1, g_loc // 2), step, 0)
 
         lax.fori_loop(0, 3, portion, 0)
         return 0
 
-    lax.fori_loop(0, nk - 1, chunk, 0)
-    stage3(nz - 2)
-    stage3(nz - 1)
-    dispatch(nk - 1)
-    lax.fori_loop(0, g_loc // 2, experts_in(nk - 1, True), 0)
+    lax.fori_loop(1, nk, chunk, 0)
+    dispatch(nz - 1, 0)
+    lax.fori_loop(0, g_loc // 2, experts_in(nk, 'last'), 0)
     hload.wait()
     pl.semaphore_signal(ready, inc=1, device_id={'ep': sib}, device_id_type=MESH)
 
@@ -449,7 +456,7 @@
         return 0
 
     lax.fori_loop(0, n2 + 3, tail_step, 0)
-    for k in range(7):
+    for k in range(1, ep):
         mcopy(k).wait_send()
 
     def drain(c, _):
@@ -485,7 +492,7 @@
             vf(ep, *meta.shape), vm(nz, ep, t, kc), vm(ep, g_loc * cp, t), vm(ep, 3 * t, g_loc * cp),
             vm(NW, 2, 2 * kc, ff), vf(g_loc, rows, ff), vf(g_loc, rows, ff), vm(g_loc, rows, 2 * kc), vm(g_loc, rows, ff),
             vm(NW2, ff, ncol), vf(n2, 2, t // 2, ncol), vf(n2, 2, t, ncol), vm(t, d),
-            dma((3,)), dma((7,)), dma((7,)), dma((nz, 8)), dma((nz, 8)), dma((NW, 2)), dma((NW2,)),
+            dma((3,)), dma((7,)), dma((7,)), dma((nz, 8)), dma((nz, 8)), dma((NW, 2, 2)), dma((NW2,)),
             dma((n2, 5)), dma((n2, 5)), dma((n2,)), pltpu.SemaphoreType.REGULAR,
         ],
         compiler_params=pltpu.CompilerParams(collective_id=0, has_side_effects=True, vmem_limit_bytes=67043328),
@@ -506,7 +513,7 @@
         top = idx.shape[-1]
         avg = top * t // (w1.shape[0] * ep)
         cap = avg + avg // 2
-        h, z, meta = attention(x.reshape(t, d), idx.reshape(t, top), gates.reshape(t, top), g1, g2, wq, wk, wv, wo, s_len, NZ, HB)
+        h, z, meta = attention(x.reshape(t, d), idx.transpose(0, 2, 1), gates.transpose(0, 2, 1), g1, g2, wq, wk, wv, wo, s_len, NZ, HB)
         return moe(ep, meta, z, h, w1, w3, w2, cap, NCOL).reshape(n, s_len, d)
 
     return jax.shard_map(body, mesh=mesh, in_specs=(tok, tok, tok, rep, rep, rep, rep, rep, rep, exs, exs, exs), out_specs=tok, check_vma=False)

time: 142 us -> 137 us (0.965)
  Pallas kernels: 137 us -> 134 us
  local copies, waits for them, and re-layouts: 4.98 us -> 2.09 us
    unnamed x3 -> x1, local copies, waits for them, and re-layouts: 4.98 us -> 2.09 us
    pallas_call x1, Pallas kernels: 120 us -> 117 us  [moe(): pl.pallas_call(functools.partial(moe_kernel, ep, (g_loc, cp, ncol)), in_s...]
where the time goes in v4:
time: 137 us; the launch traced here: 136 us
  Pallas kernels  134 us (98%)
  local copies, waits for them, and re-layouts  2.09 us (2%)
    pallas_call x1, Pallas kernels, moe(): pl.pallas_call(functools.partial(moe_kernel, ep, (g_loc, cp, ncol)), in_s...  117 us
    pallas_call x1, Pallas kernels, attention(): pl.pallas_call(functools.partial(attn_kernel, hb, seq), grid=(wid // c,),...  17.4 us

profile of v4, /device:TPU:112, one launch (start us, length us, event | category | flops | bytes accessed | tf_op | source)
XLA Modules:
  0.0 136.4 jit_solution(3056507477000570870)
XLA Ops:
  0.0 17.4 %attention.1 = (bf16[192,2048]{1,0:T(8,128)(2,1)}, bf16[8,192,256]{2,1,0:T(8,128)(2,1)}, f32[16,256]{1,0:T(8,128)}) custom-call(bf16[192,2048]{1,0:T(8,128)(2,1)} %bitcast.7, s32[3,8,64]{2,1,0:T(8,128)} %bitcast.8, f32[3,8,64]{2,1,0:T(8,128)} %bitcast.9, f32[1,2048]{1,0:T(1,128)} %bitcast.10, f32[1,2048]{1,0:T(1,128)} %bitcast.11, ...), custom_call_target="tpu_custom_call" | custom-call | flops 6442450944 | bytes 33554432 | tf_op jit(solution)/shard_map/attention/pallas_call | solution.py:80
  17.4 116.9 %moe.1 = bf16[192,2048]{1,0:T(8,128)(2,1)} custom-call(f32[16,256]{1,0:T(8,128)} %get-tuple-element.8.meta_ref, bf16[8,192,256]{2,1,0:T(8,128)(2,1)} %get-tuple-element.9.z_ref, bf16[192,2048]{1,0:T(8,128)(2,1)} %get-tuple-element.10.h_hbm, bf16[8,2048,1024]{2,1,0:T(8,128)(2,1)} %w1_ref.1, bf16[8,2048,1024]{2,1,0:T(8,128)(2,1)} %w3_ref.1, ...), custom_call_target="tpu_custom_call" | custom-call | flops 32212254720 | bytes 100663296 | tf_op jit(solution)/shard_map/moe/pallas_call | solution.py:486
  134.3 2.1 %copy.14 = bf16[3,64,2048]{2,1,0:T(8,128)(2,1)} copy(bf16[3,64,2048]{2,1,0:T(8,128)(2,1)} %bitcast.6) | data formatting | bytes 1572864

commit v5 on v4

--- a/solution.py
+++ b/solution.py
@@ -23,92 +23,13 @@
     return hi, mid, (r - mid.astype(F32)).astype(BF16)
 
 
-def attn_kernel(hb, seq, x_ref, idx_ref, gate_ref, g1_ref, g2_ref, wq_ref, wk_ref, wv_ref, wo_ref, h_ref, z_ref, meta_ref, xn_ref, acc_ref):
-    i = pl.program_id(0)
-    t = x_ref.shape[0]
-
-    @pl.when(i == 0)
-    def _():
-        xn_ref[...] = rms(x_ref[...].astype(F32), g1_ref[...])
-        acc_ref[...] = jnp.zeros_like(acc_ref)
-        top, tp = meta_ref.shape[0] // 2, meta_ref.shape[1]
-        ids, gts = jnp.zeros((top, tp), F32), jnp.zeros((top, tp), F32)
-        for n in range(t // seq):
-            at, to = lax.broadcasted_iota(jnp.int32, (seq, tp), 0), lax.broadcasted_iota(jnp.int32, (seq, tp), 1)
-            move = jnp.where(at + n * seq == to, 1.0, 0.0).astype(BF16)
-            ids += jnp.dot(idx_ref[n].astype(F32).astype(BF16), move, preferred_element_type=F32)
-            hi, mid, lo = [jnp.dot(p, move, preferred_element_type=F32) for p in split3(gate_ref[n])]
-            gts += hi + mid + lo
-        meta_ref[:top] = jnp.where(lax.broadcasted_iota(jnp.int32, (top, tp), 1) < t, ids, -1.0)
-        meta_ref[top:] = gts
-
-    xn = xn_ref[...]
-    q = jnp.dot(xn, wq_ref[...], preferred_element_type=F32).astype(BF16)
-    k = jnp.dot(xn, wk_ref[...], preferred_element_type=F32).astype(BF16)
-    v = jnp.dot(xn, wv_ref[...], preferred_element_type=F32).astype(BF16)
-    row = lax.broadcasted_iota(jnp.int32, (t, t), 0)
-    col = lax.broadcasted_iota(jnp.int32, (t, t), 1)
-    mask = (row >= col) & (row // seq == col // seq)
-    outs = []
-    for j in range(hb):
-        sl = slice(j * HEAD, (j + 1) * HEAD)
-        s = lax.dot_general(q[:, sl], k[:, sl], (((1,), (1,)), ((), ())), preferred_element_type=F32) * HEAD ** -0.5
-        s = jnp.where(mask, s, -1e30)
-        e = jnp.exp(s - jnp.max(s, axis=-1, keepdims=True))
-        p = (e / jnp.sum(e, axis=-1, keepdims=True)).astype(BF16)
-        outs.append(jnp.dot(p, v[:, sl], preferred_element_type=F32).astype(BF16))
-    o = jnp.concatenate(outs, axis=1)
-    acc_ref[...] += jnp.dot(o, wo_ref[...], preferred_element_type=F32)
-
-    @pl.when(i == pl.num_programs(0) - 1)
-    def _():
-        att = acc_ref[...].astype(BF16)
-        h = (x_ref[...].astype(F32) + att.astype(F32)).astype(BF16)
-        h_ref[...] = h
-        z = rms(h.astype(F32), g2_ref[...])
-        kc = z_ref.shape[2]
-        for c in range(z_ref.shape[0]):
-            z_ref[c] = z[:, c * kc:(c + 1) * kc]
-
-
-def attention(xf, idx, gates, g1, g2, wq, wk, wv, wo, seq, nz, hb):
-    t, d = xf.shape
-    n, top, _ = idx.shape
-    tp = t + -t % 128
-    wid = wq.shape[1]
-    c = hb * HEAD
-    return pl.pallas_call(
-        functools.partial(attn_kernel, hb, seq),
-        grid=(wid // c,),
-        in_specs=[
-            pl.BlockSpec((t, d), lambda i: (0, 0)),
-            pl.BlockSpec((n, top, seq), lambda i: (0, 0, 0)),
-            pl.BlockSpec((n, top, seq), lambda i: (0, 0, 0)),
-            pl.BlockSpec((1, d), lambda i: (0, 0)),
-            pl.BlockSpec((1, d), lambda i: (0, 0)),
-            pl.BlockSpec((d, c), lambda i: (0, i)),
-            pl.BlockSpec((d, c), lambda i: (0, i)),
-            pl.BlockSpec((d, c), lambda i: (0, i)),
-            pl.BlockSpec((c, d), lambda i: (i, 0)),
-        ],
-        out_specs=[pl.BlockSpec((t, d), lambda i: (0, 0)), pl.BlockSpec((nz, t, d // nz), lambda i: (0, 0, 0)),
-                   pl.BlockSpec((2 * top, tp), lambda i: (0, 0))],
-        out_shape=[jax.ShapeDtypeStruct((t, d), BF16), jax.ShapeDtypeStruct((nz, t, d // nz), BF16),
-                   jax.ShapeDtypeStruct((2 * top, tp), F32)],
-        scratch_shapes=[pltpu.VMEM((t, d), BF16), pltpu.VMEM((t, d), F32)],
-        compiler_params=pltpu.CompilerParams(dimension_semantics=("arbitrary",), vmem_limit_bytes=67043328),
-        cost_estimate=pl.CostEstimate(flops=8 * t * d * wid, bytes_accessed=8 * d * wid, transcendentals=0),
-        name="attention",
-    )(xf, idx, gates, g1.reshape(1, d), g2.reshape(1, d), wq, wk, wv, wo)
-
-
 MESH = pl.DeviceIdType.MESH
 NZ, NW, NW2, NCOL, HB = 8, 6, 8, 256, 4
 
 
-def moe_kernel(ep, cfg, meta_ref, z_ref, h_hbm, w1_ref, w3_ref, w2_ref, y_ref,
-               mbuf, zbuf, dbuf, gbuf, wbuf, acc1, acc3, rbuf, ubuf, w2buf, h1buf, h2buf, h_ref,
-               load_sem, m_send, m_recv, z_send, z_recv, w_sem, w2_sem, r_send, r_recv, y_sem, ready):
+def layer_kernel(ep, cfg, x_ref, idx_hbm, gate_hbm, g1_hbm, g2_hbm, wq_ref, wk_ref, wv_ref, wo_ref, w1_ref, w3_ref, w2_ref, y_ref,
+                 idx_ref, gate_ref, g1_ref, g2_ref, mbuf, zbuf, dbuf, gbuf, wbuf, acc1, acc3, rbuf, ubuf, w2buf, h1buf, h2buf, h_ref,
+                 load_sem, m_send, m_recv, z_send, z_recv, w_sem, w2_sem, r_send, r_recv, y_sem, ready):
     g_loc, cp, ncol = cfg
     nz, _, t, kc = zbuf.shape
     tp = mbuf.shape[2]
@@ -122,6 +43,9 @@
     n2 = d // ncol
     nq = ff // ncol
     fit = (rows - t) // cp
+    hbw = HB * HEAD
+    blocks = wq_ref.shape[1] // hbw
+    assert d == 2 * ff and hbw == kw and ff == 2 * kw
     assert fit * nq >= ep
     nw, nw2 = wbuf.shape[0], w2buf.shape[0]
 
@@ -137,7 +61,7 @@
     def wcopy(n, which, unit):
         e, c = lax.rem(n, g_loc), n // g_loc
         ref = w3_ref if which else w1_ref
-        slot = lax.rem(n, nw)
+        slot = lax.rem(n + 4 * blocks, nw)
         row = pl.multiple_of((jnp.maximum(2 * c - 1, 0) + unit) * kc, kc)
         return pltpu.make_async_copy(ref.at[e, pl.ds(row, kc)], wbuf.at[slot, which, unit * kc:(unit + 1) * kc],
                                      w_sem.at[slot, which, unit])
@@ -158,22 +82,37 @@
         slot = lax.rem(n, nw2)
         return pltpu.make_async_copy(w2_ref.at[e, :, pl.ds(pl.multiple_of(c * ncol, ncol), ncol)], w2buf.at[slot], w2_sem.at[slot])
 
-    zload = pltpu.make_async_copy(z_ref, zbuf.at[:, me], load_sem.at[0])
-    mload = pltpu.make_async_copy(meta_ref, mbuf.at[me], load_sem.at[1])
-    hload = pltpu.make_async_copy(h_hbm, h_ref, load_sem.at[2])
-    zload.start()
-    mload.start()
-    hload.start()
-    for n in range(nw):
-        wstart(n)
-    for n in range(nw2):
-        w2copy(n).start()
+    loads = [pltpu.make_async_copy(src, dst, load_sem.at[k]) for k, (src, dst) in enumerate((
+        (idx_hbm, idx_ref), (gate_hbm, gate_ref), (x_ref, h_ref), (g1_hbm, g1_ref), (g2_hbm, g2_ref)))]
+
+    def acopies(l):
+        b, which, slot = l // 4, l % 4, l % nw
+        at = slice(b * hbw, (b + 1) * hbw)
+        if which == 3:
+            return [pltpu.make_async_copy(wo_ref.at[at, a * ff:(a + 1) * ff], wbuf.at[slot, a], w_sem.at[slot, a, 0]) for a in range(2)]
+        ref = (wq_ref, wk_ref, wv_ref)[which]
+        return [pltpu.make_async_copy(ref.at[j * kw:(j + 1) * kw, at], wbuf.at[slot, j // 2, :, j % 2 * hbw:(j % 2 + 1) * hbw],
+                                      w_sem.at[slot, j // 2, j % 2]) for j in range(4)]
+
+    def lstart(l):
+        if l < 4 * blocks:
+            for copy in acopies(l):
+                copy.start()
+        else:
+            wstart(jnp.int32(l - 4 * blocks))
+
+    def lwait(l):
+        for copy in acopies(l):
+            copy.wait()
+
+    for copy in loads:
+        copy.start()
+    for l in range(nw):
+        lstart(l)
 
     barrier = pltpu.get_barrier_semaphore()
     for k in range(1, ep):
         pl.semaphore_signal(barrier, inc=1, device_id={'ep': lax.rem(me + k, ep)}, device_id_type=MESH)
-    mload.wait()
-    pl.semaphore_wait(barrier, ep - 1)
 
     def mcopy(k):
         return send(mbuf.at[me], mbuf.at[me], m_send.at[k - 1], m_recv.at[k - 1], lax.rem(me + k, ep))
@@ -223,9 +162,66 @@
         def _():
             stage2(m)
 
+    loads[0].wait()
+    loads[1].wait()
+    seqs, top, seq = idx_ref.shape
+    ids, gts = jnp.zeros((top, tp), F32), jnp.zeros((top, tp), F32)
+    for n in range(seqs):
+        at, to = lax.broadcasted_iota(jnp.int32, (seq, tp), 0), lax.broadcasted_iota(jnp.int32, (seq, tp), 1)
+        move = jnp.where(at + n * seq == to, 1.0, 0.0).astype(BF16)
+        ids += jnp.dot(idx_ref[n].astype(F32).astype(BF16), move, preferred_element_type=F32)
+        hi, mid, lo = [jnp.dot(p, move, preferred_element_type=F32) for p in split3(gate_ref[n])]
+        gts += hi + mid + lo
+    mbuf[me, :top] = jnp.where(lax.broadcasted_iota(jnp.int32, (top, tp), 1) < t, ids, -1.0)
+    mbuf[me, top:] = gts
+
+    for k in (2, 3, 4):
+        loads[k].wait()
+    xn = rms(h_ref[...].astype(F32), g1_ref[...])
+    for a in range(2):
+        ubuf[a, :t] = xn[:, a * ff:(a + 1) * ff]
+    pl.semaphore_wait(barrier, ep - 1)
     for k in range(1, ep):
         mcopy(k).start()
-    zload.wait()
+
+    row = lax.broadcasted_iota(jnp.int32, (t, t), 0)
+    col = lax.broadcasted_iota(jnp.int32, (t, t), 1)
+    mask = (row >= col) & (row // seq == col // seq)
+
+    def project(l):
+        slot = l % nw
+        parts = [jnp.dot(ubuf[j // 2, :t, j % 2 * kw:(j % 2 + 1) * kw], wbuf[slot, j // 2, :, j % 2 * hbw:(j % 2 + 1) * hbw],
+                         preferred_element_type=F32) for j in range(4)]
+        return (parts[0] + parts[1] + parts[2] + parts[3]).astype(BF16)
+
+    for b in range(blocks):
+        for k in range(3):
+            lwait(4 * b + k)
+        q, k, v = [project(4 * b + i) for i in range(3)]
+        for i in range(3):
+            lstart(4 * b + i + nw)
+        outs = []
+        for j in range(HB):
+            sl = slice(j * HEAD, (j + 1) * HEAD)
+            s = lax.dot_general(q[:, sl], k[:, sl], (((1,), (1,)), ((), ())), preferred_element_type=F32) * HEAD ** -0.5
+            s = jnp.where(mask, s, -1e30)
+            e = jnp.exp(s - jnp.max(s, axis=-1, keepdims=True))
+            p = (e / jnp.sum(e, axis=-1, keepdims=True)).astype(BF16)
+            outs.append(jnp.dot(p, v[:, sl], preferred_element_type=F32).astype(BF16))
+        o = jnp.concatenate(outs, axis=1)
+        lwait(4 * b + 3)
+        for a in range(2):
+            part = jnp.dot(o, wbuf[(4 * b + 3) % nw, a], preferred_element_type=F32)
+            acc1[a, :t] = part if b == 0 else acc1[a, :t] + part
+        lstart(4 * b + 3 + nw)
+
+    h = (h_ref[...].astype(F32) + jnp.concatenate([acc1[0, :t], acc1[1, :t]], axis=1).astype(BF16).astype(F32)).astype(BF16)
+    h_ref[...] = h
+    z = rms(h.astype(F32), g2_ref[...])
+    for m in range(nz):
+        zbuf[m, me] = z[:, m * kc:(m + 1) * kc]
+    for n in range(nw2):
+        w2copy(n).start()
     own(0)
     own(1)
     for k in range(1, ep):
@@ -261,9 +257,9 @@
             gbuf[s, i * t:(i + 1) * t] = jnp.where(sel, widen(part), 0.0).astype(BF16)
 
     def builds(i, _):
-        hop(i)
         for q in range(4):
             build(4 * i + q)
+        hop(i)
         return 0
 
     lax.fori_loop(0, ep // 4, builds, 0)
@@ -290,7 +286,7 @@
                     wcopy(n + q, 0, u).wait()
                     wcopy(n + q, 1, u).wait()
             for q in range(2):
-                e, slot = 2 * i + q, lax.rem(n + q, nw)
+                e, slot = 2 * i + q, lax.rem(n + q + 4 * blocks, nw)
                 r = rbuf[e, :, :k]
                 a = jnp.dot(r, wbuf[slot, 0, :k], preferred_element_type=F32)
                 b = jnp.dot(r, wbuf[slot, 1, :k], preferred_element_type=F32)
@@ -344,7 +340,6 @@
     lax.fori_loop(1, nk, chunk, 0)
     dispatch(nz - 1, 0)
     lax.fori_loop(0, g_loc // 2, experts_in(nk, 'last'), 0)
-    hload.wait()
     pl.semaphore_signal(ready, inc=1, device_id={'ep': sib}, device_id_type=MESH)
 
     def cols(c):
@@ -473,9 +468,10 @@
     lax.fori_loop(0, n2, finish, 0)
 
 
-def moe(ep, meta, z, h, w1, w3, w2, cap, ncol):
-    nz, t, kc = z.shape
-    g_loc, d, ff = w1.shape
+def layer(ep, x, idx, gates, g1, g2, wq, wk, wv, wo, w1, w3, w2, cap, ncol):
+    t, d = x.shape
+    g_loc, _, ff = w1.shape
+    nz, kc, tp, top = NZ, d // NZ, t + -t % 128, idx.shape[1]
     cp = -(-cap // 8) * 8
     rows = ep * cp
     n2 = d // ncol
@@ -484,21 +480,21 @@
     hbm = pl.BlockSpec(memory_space=pltpu.HBM)
     dma = pltpu.SemaphoreType.DMA
     return pl.pallas_call(
-        functools.partial(moe_kernel, ep, (g_loc, cp, ncol)),
-        in_specs=[hbm] * 6,
+        functools.partial(layer_kernel, ep, (g_loc, cp, ncol)),
+        in_specs=[hbm] * 12,
         out_specs=hbm,
         out_shape=jax.ShapeDtypeStruct((t, d), BF16),
         scratch_shapes=[
-            vf(ep, *meta.shape), vm(nz, ep, t, kc), vm(ep, g_loc * cp, t), vm(ep, 3 * t, g_loc * cp),
+            pltpu.VMEM(idx.shape, jnp.int32), vf(*gates.shape), vf(1, d), vf(1, d), vf(ep, 2 * top, tp), vm(nz, ep, t, kc), vm(ep, g_loc * cp, t), vm(ep, 3 * t, g_loc * cp),
             vm(NW, 2, 2 * kc, ff), vf(g_loc, rows, ff), vf(g_loc, rows, ff), vm(g_loc, rows, 2 * kc), vm(g_loc, rows, ff),
             vm(NW2, ff, ncol), vf(n2, 2, t // 2, ncol), vf(n2, 2, t, ncol), vm(t, d),
-            dma((3,)), dma((7,)), dma((7,)), dma((nz, 8)), dma((nz, 8)), dma((NW, 2, 2)), dma((NW2,)),
+            dma((5,)), dma((ep - 1,)), dma((ep - 1,)), dma((nz, 8)), dma((nz, 8)), dma((NW, 2, 2)), dma((NW2,)),
             dma((n2, 5)), dma((n2, 5)), dma((n2,)), pltpu.SemaphoreType.REGULAR,
         ],
         compiler_params=pltpu.CompilerParams(collective_id=0, has_side_effects=True, vmem_limit_bytes=67043328),
         cost_estimate=pl.CostEstimate(flops=6 * g_loc * rows * d * ff, bytes_accessed=6 * g_loc * d * ff, transcendentals=0),
-        name="moe",
-    )(meta, z, h, w1, w3, w2)
+        name="layer",
+    )(x, idx, gates, g1.reshape(1, d), g2.reshape(1, d), wq, wk, wv, wo, w1, w3, w2)
 
 
 def solution(mesh):
@@ -513,7 +509,7 @@
         top = idx.shape[-1]
         avg = top * t // (w1.shape[0] * ep)
         cap = avg + avg // 2
-        h, z, meta = attention(x.reshape(t, d), idx.transpose(0, 2, 1), gates.transpose(0, 2, 1), g1, g2, wq, wk, wv, wo, s_len, NZ, HB)
-        return moe(ep, meta, z, h, w1, w3, w2, cap, NCOL).reshape(n, s_len, d)
+        y = layer(ep, x.reshape(t, d), idx.transpose(0, 2, 1), gates.transpose(0, 2, 1), g1, g2, wq, wk, wv, wo, w1, w3, w2, cap, NCOL)
+        return y.reshape(n, s_len, d)
 
     return jax.shard_map(body, mesh=mesh, in_specs=(tok, tok, tok, rep, rep, rep, rep, rep, rep, exs, exs, exs), out_specs=tok, check_vma=False)

time: 137 us -> 132 us (0.964)
  Pallas kernels: 134 us -> 130 us
    pallas_call x2 -> x1, Pallas kernels: 134 us -> 130 us  [layer(): pl.pallas_call(functools.partial(layer_kernel, ep, (g_loc, cp, ncol)), in...]
where the time goes in v5:
time: 132 us
  Pallas kernels  130 us (98%)
  local copies, waits for them, and re-layouts  2.09 us (2%)
    pallas_call x1, Pallas kernels, layer(): pl.pallas_call(functools.partial(layer_kernel, ep, (g_loc, cp, ncol)), in...  130 us

profile of v5, /device:TPU:112, one launch (start us, length us, event | category | flops | bytes accessed | tf_op | source)
XLA Modules:
  0.0 131.9 jit_solution(12327406231580894706)
XLA Ops:
  0.0 129.8 %layer.1 = bf16[192,2048]{1,0:T(8,128)(2,1)} custom-call(bf16[192,2048]{1,0:T(8,128)(2,1)} %bitcast.7, s32[3,8,64]{2,1,0:T(8,128)} %bitcast.8, f32[3,8,64]{2,1,0:T(8,128)} %bitcast.9, f32[1,2048]{1,0:T(1,128)} %bitcast.10, f32[1,2048]{1,0:T(1,128)} %bitcast.11, bf16[2048,2048]{1,0:T(8,128)(2,1)} %wq_ref.1, bf16[2048,2048]{1,0:T(8,128)(2,1)} %wk_ref.1, ...), custom_call_target="tpu_custom_call" | custom-call | flops 32212254720 | bytes 100663296 | tf_op jit(solution)/shard_map/layer/pallas_call | solution.py:482
  129.8 2.1 %copy.14 = bf16[3,64,2048]{2,1,0:T(8,128)(2,1)} copy(bf16[3,64,2048]{2,1,0:T(8,128)(2,1)} %bitcast.6) | data formatting | bytes 1572864
